TPU v7x, 256 devices: a whole 4x4x8 slice. The times are simulated.
256 devices in a mesh: blk: 16 (over z, y_lo), grp: 16 (over x, y_hi, core).
Axes of the slice: x: 4, y: 4 (y_hi: 2, y_lo: 2; y = y_hi * 2 + y_lo), z: 8, core: 2. Of those that a mesh axis runs over, the one named last changes fastest.
Arguments:
- frames: bfloat16 [16, 4096, 1024], P('grp', 'blk'), may hold values from -16 to 16
- utt_lengths: int32 [8], replicated, may hold values from 1 to 16384, 65536 in all
- attn_gain: float32 [1024], replicated, may hold values from 0.25 to 1.75
- w_qkv: bfloat16 [1024, 3072], P(None, 'grp'), may hold values from -4 to 4
- w_out: bfloat16 [1024, 1024], replicated, may hold values from -0.375 to 0.375
- conv_gain: float32 [1024], replicated, may hold values from 0.25 to 1.75
- w_glu: bfloat16 [1024, 2048], replicated, may hold values from -0.1875 to 0.1875
- w_depth: float32 [31, 1024], replicated, may hold values from -1 to 1
- depth_gain: float32 [1024], replicated, may hold values from 0.25 to 1.75
- w_proj: bfloat16 [1024, 1024], replicated, may hold values from -0.1875 to 0.1875
Outputs:
- block_out: bfloat16 [16, 4096, 1024], P('grp', 'blk')
Inputs may be any that keep to these rules, and one draw needn't show every extreme that they name: `utt_lengths`: they sum to 65536 and the longest is exactly 16384.
All inputs are finite; a program needn't handle non-finite values.
Results may differ from a plain program's by a relative error of at most 0.0095.
Values may be sent and summed in bfloat16 or wider, within the bound.
A program may use at most 192 MiB of HBM per device.

v0:
```python
import jax
import jax.numpy as jnp
from jax import lax
from jax.sharding import PartitionSpec as P

HEADS = 16


epsilon = 1e-05
big_negative = -1e30


def padded_2(block, sides, width, periodic):
    for axis, dim in sides:
        count = lax.axis_size(axis)
        forward = [(i, i + 1) for i in range(count - 1)]
        if periodic:
            forward.append((count - 1, 0))
        backward = [(target, source) for source, target in forward]
        low = lax.ppermute(
            lax.slice_in_dim(block, block.shape[dim] - width, None, axis=dim), axis, forward
        )
        high = lax.ppermute(lax.slice_in_dim(block, 0, width, axis=dim), axis, backward)
        block = jnp.concatenate([low, block, high], axis=dim)
    return block


def normalize(values, row_gain):
    center = values - jnp.mean(values, axis=-1, keepdims=True)
    spread = jnp.mean(center * center, axis=-1, keepdims=True)
    return center * lax.rsqrt(spread + epsilon) * row_gain


def segment_of(utt_lengths, positions):
    starts = jnp.cumsum(utt_lengths) - utt_lengths
    started = (starts[None, :] <= positions[:, None]).astype(jnp.int32)
    return jnp.sum(started, axis=1) - 1


def body(
    frames, utt_lengths, attn_gain, w_qkv, w_out, conv_gain, w_glu, w_depth, depth_gain, w_proj
):
    frame_rows = frames.shape[1]
    width = frames.shape[2]
    head_count = HEADS
    head_width = width // head_count
    kernel_half = (w_depth.shape[0] - 1) // 2
    score_scale = head_width ** (-0.5)
    blocks = lax.axis_size("blk")
    block_index = lax.axis_index("blk")
    group_index = lax.axis_index("grp")
    window = frame_rows * blocks
    window_start = group_index * window
    first_frame = window_start + block_index * frame_rows
    local_frames = frames[0]
    local_float = local_frames.astype(jnp.float32)
    normed = normalize(local_float, attn_gain).astype(jnp.bfloat16)
    qkv_rows = jnp.dot(
        normed, lax.all_gather(w_qkv, "grp", axis=1, tiled=True), preferred_element_type=jnp.float32
    ).astype(jnp.bfloat16)
    local_seg = segment_of(utt_lengths, first_frame + jnp.arange(frame_rows, dtype=jnp.int32))
    my_heads = lax.all_to_all(qkv_rows, "blk", split_axis=1, concat_axis=0, tiled=True)
    local_heads = head_count // blocks
    qkv_split = my_heads.reshape(window, local_heads, 3, head_width)
    query_all = qkv_split[:, :, 0, :]
    keys_all = qkv_split[:, :, 1, :]
    values_all = qkv_split[:, :, 2, :]
    window_seg = segment_of(utt_lengths, window_start + jnp.arange(window, dtype=jnp.int32))
    query_block = min(512, window)
    block_count = window // query_block

    def attend(block_id):
        block_start = block_id * query_block
        queries = lax.dynamic_slice_in_dim(query_all, block_start, query_block, 0)
        query_seg = lax.dynamic_slice_in_dim(window_seg, block_start, query_block, 0)
        allowed = (query_seg[:, None] == window_seg[None, :])[None]
        scores = (
            jnp.einsum("qhd,khd->hqk", queries, keys_all, preferred_element_type=jnp.float32)
            * score_scale
        )
        row_max = jnp.max(jnp.where(allowed, scores, big_negative), axis=2, keepdims=True)
        weights = jnp.where(allowed, jnp.exp(scores - row_max), 0.0)
        row_total = jnp.sum(weights, axis=2)
        mixed_values = jnp.einsum(
            "hqk,khd->qhd",
            weights.astype(jnp.bfloat16),
            values_all,
            preferred_element_type=jnp.float32,
        )
        normed_values = mixed_values / jnp.transpose(row_total)[:, :, None]
        return normed_values.reshape(query_block, local_heads * head_width).astype(jnp.bfloat16)

    pieces = lax.map(attend, jnp.arange(block_count, dtype=jnp.int32))
    merged_heads = pieces.reshape(window, local_heads * head_width)
    attended = lax.all_to_all(merged_heads, "blk", split_axis=0, concat_axis=1, tiled=True)
    residual = (local_float + jnp.dot(attended, w_out, preferred_element_type=jnp.float32)).astype(
        jnp.bfloat16
    )
    residual = lax.optimization_barrier(residual)
    conv_in = normalize(residual.astype(jnp.float32), conv_gain).astype(jnp.bfloat16)
    projected = jnp.dot(conv_in, w_glu, preferred_element_type=jnp.float32)
    gated = (projected[:, :width] * jax.nn.sigmoid(projected[:, width:])).astype(jnp.bfloat16)
    gated = lax.optimization_barrier(gated)
    padded = padded_2(gated, (("blk", 0),), kernel_half, True)
    left_rim = padded[:kernel_half]
    right_rim = padded[frame_rows + kernel_half :]
    outer_rims = padded_2(jnp.stack([right_rim, left_rim]), (("grp", 0),), 1, False)
    left_edge = jnp.where(block_index == 0, outer_rims[0], left_rim)
    right_edge = jnp.where(block_index == blocks - 1, outer_rims[3], right_rim)
    extended = jnp.concatenate([left_edge, gated, right_edge], axis=0).astype(jnp.float32)
    extended_seg = segment_of(
        utt_lengths,
        first_frame - kernel_half + jnp.arange(frame_rows + 2 * kernel_half, dtype=jnp.int32),
    )
    mixed_conv = jnp.zeros((frame_rows, width), jnp.float32)
    for offset in range(2 * kernel_half + 1):
        same_seg = (extended_seg[offset : offset + frame_rows] == local_seg)[:, None]
        mixed_conv = mixed_conv + jnp.where(
            same_seg, extended[offset : offset + frame_rows] * w_depth[offset], 0.0
        )
    normed_conv = normalize(mixed_conv, depth_gain)
    activated = (normed_conv * jax.nn.sigmoid(normed_conv)).astype(jnp.bfloat16)
    result = (
        residual.astype(jnp.float32)
        + jnp.dot(activated, w_proj, preferred_element_type=jnp.float32)
    ).astype(jnp.bfloat16)
    return result[None]


def solution(mesh):
    in_specs = (P("grp", "blk", None), P(), P(), P(None, "grp"), P(), P(), P(), P(), P(), P())
    out_specs = P("grp", "blk", None)
    return jax.shard_map(body, mesh=mesh, in_specs=in_specs, out_specs=out_specs, check_vma=False)
```

profile of v0, /device:TPU:1, one launch (start us, length us, event | category | flops | bytes accessed | tf_op | source)
XLA Modules:
  0.0 285.7 jit_solution(17601344647619971981)
XLA Ops:
  9.8 73.4 %all-gather.2.cloned.1.call-done = bf16[1024,3072]{0,1:T(8,128)(2,1)} async-done(((bf16[1024,192]{0,1:T(8,128)(2,1)}), bf16[1024,3072]{0,1:T(8,128)(2,1)}) %all-gather.2.cloned.1.call-update) | async-done | bytes 6291472 | tf_op jit(solution)/shard_map/all_gather | solution.py:59
  83.2 6.0 %convolution_convert_fusion = bf16[256,3072]{1,0:T(8,128)(2,1)} fusion(bf16[1024,3072]{0,1:T(8,128)(2,1)} %all-gather.2.cloned.1.call-done, bf16[1,256,1024]{2,1,0:T(8,128)(2,1)} %param.12, f32[1024]{0:T(1024)} %param.14, f32[256]{0:T(256)S(1)} %add_rsqrt_fusion.2, f32[256]{0:T(256)S(1)} %broadcast_multiply_fusion.2), kind=kOutput, calls=%fused_computation.19 | convolution fusion | flops 1612709888 | bytes 8394752 | tf_op jit(solution)/shard_map/dot_general | solution.py:58
  91.8 6.9 %all-to-all-start = ((bf16[256,16,192]{0,2,1:T(8,128)(2,1)}), bf16[256,16,192]{0,2,1:T(8,128)(2,1)}, u32[]{:S(2)}, u32[]{:S(2)}) async-start(bf16[256,16,192]{0,2,1:T(8,128)(2,1)} %bitcast.125), calls=%async_computation | async-start | bytes 3145728 | tf_op jit(solution)/shard_map/all_to_all | solution.py:62
  99.1 35.8 %all-to-all-done = bf16[256,16,192]{0,2,1:T(8,128)(2,1)} async-done(((bf16[256,16,192]{0,2,1:T(8,128)(2,1)}), bf16[256,16,192]{0,2,1:T(8,128)(2,1)}, u32[]{:S(2)}, u32[]{:S(2)}) %all-to-all-start) | async-done | bytes 1572896 | tf_op jit(solution)/shard_map/all_to_all | solution.py:62
  134.8 3.4 %copy.20 = bf16[16,256,192]{1,0,2:T(8,128)(2,1)} copy(bf16[16,256,192]{1,2,0:T(8,128)(2,1)} %bitcast.12) | data formatting | bytes 3145728 | tf_op jit(solution)/shard_map/all_to_all | solution.py:62
  138.3 3.8 %reshape.169 = bf16[4096,1,3,64]{0,3,2,1:T(8,128)(2,1)} reshape(bf16[16,256,192]{1,0,2:T(8,128)(2,1)} %copy.20) | data formatting | bytes 3145728 | tf_op jit(solution)/shard_map/reshape | solution.py:64
  144.5 75.0 %while.10 = (s32[]{:T(128)}, bf16[8,512,64]{1,2,0:T(8,128)(2,1)}, s32[8]{0:T(128)S(1)}, s32[4096]{0:T(1024)S(1)}, bf16[4096,1,64]{0,2,1:T(8,128)(2,1)}, /*index=...) while((s32[]{:T(128)}, bf16[8,512,64]{1,2,0:T(8,128)(2,1)}, ...), condition=%wide.region_7.8_spmd, body=%wide.region_4.0_spmd.sunk | while | flops 566295552 | bytes 26415792 | solution.py:93
  150.9 3.0 %fusion.141 = bf16[8,512,64]{1,2,0:T(8,128)(2,1)} fusion(bf16[8,512,64]{1,2,0:T(8,128)(2,1)} %get-tuple-element.187, s32[]{:T(128)} %get-tuple-element.186, f32[512,4096]{1,0:T(8,128)S(1)} %get-tuple-element.173, f32[512]{0:T(512)S(1)} %get-tuple-element.174, s32[4096]{0:T(1024)S(1)} %get-tuple-element.200, s32[512]{0:T(512)S(1)} %dynamic_slice.21, ...), kind=kOutput, calls=%fused_computation.10.clone.1 | convolution fusion | flops 278986752 | bytes 9001472 | tf_op jit(solution)/shard_map/while/body/eval_jaxpr/hqk,khd->qhd/dot_general | solution.py:84
  160.3 3.0 %fusion.141 = bf16[8,512,64]{1,2,0:T(8,128)(2,1)} fusion(bf16[8,512,64]{1,2,0:T(8,128)(2,1)} %get-tuple-element.187, s32[]{:T(128)} %get-tuple-element.186, f32[512,4096]{1,0:T(8,128)S(1)} %get-tuple-element.173, f32[512]{0:T(512)S(1)} %get-tuple-element.174, s32[4096]{0:T(1024)S(1)} %get-tuple-element.200, s32[512]{0:T(512)S(1)} %dynamic_slice.21, ...), kind=kOutput, calls=%fused_computation.10.clone.1 | convolution fusion | flops 278986752 | bytes 9001472 | tf_op jit(solution)/shard_map/while/body/eval_jaxpr/hqk,khd->qhd/dot_general | solution.py:84
  164.6 2.7 fusion.139
  169.7 3.0 %fusion.141 = bf16[8,512,64]{1,2,0:T(8,128)(2,1)} fusion(bf16[8,512,64]{1,2,0:T(8,128)(2,1)} %get-tuple-element.187, s32[]{:T(128)} %get-tuple-element.186, f32[512,4096]{1,0:T(8,128)S(1)} %get-tuple-element.173, f32[512]{0:T(512)S(1)} %get-tuple-element.174, s32[4096]{0:T(1024)S(1)} %get-tuple-element.200, s32[512]{0:T(512)S(1)} %dynamic_slice.21, ...), kind=kOutput, calls=%fused_computation.10.clone.1 | convolution fusion | flops 278986752 | bytes 9001472 | tf_op jit(solution)/shard_map/while/body/eval_jaxpr/hqk,khd->qhd/dot_general | solution.py:84
  179.1 3.0 %fusion.141 = bf16[8,512,64]{1,2,0:T(8,128)(2,1)} fusion(bf16[8,512,64]{1,2,0:T(8,128)(2,1)} %get-tuple-element.187, s32[]{:T(128)} %get-tuple-element.186, f32[512,4096]{1,0:T(8,128)S(1)} %get-tuple-element.173, f32[512]{0:T(512)S(1)} %get-tuple-element.174, s32[4096]{0:T(1024)S(1)} %get-tuple-element.200, s32[512]{0:T(512)S(1)} %dynamic_slice.21, ...), kind=kOutput, calls=%fused_computation.10.clone.1 | convolution fusion | flops 278986752 | bytes 9001472 | tf_op jit(solution)/shard_map/while/body/eval_jaxpr/hqk,khd->qhd/dot_general | solution.py:84
  183.3 2.7 fusion.139
  188.4 3.0 %fusion.141 = bf16[8,512,64]{1,2,0:T(8,128)(2,1)} fusion(bf16[8,512,64]{1,2,0:T(8,128)(2,1)} %get-tuple-element.187, s32[]{:T(128)} %get-tuple-element.186, f32[512,4096]{1,0:T(8,128)S(1)} %get-tuple-element.173, f32[512]{0:T(512)S(1)} %get-tuple-element.174, s32[4096]{0:T(1024)S(1)} %get-tuple-element.200, s32[512]{0:T(512)S(1)} %dynamic_slice.21, ...), kind=kOutput, calls=%fused_computation.10.clone.1 | convolution fusion | flops 278986752 | bytes 9001472 | tf_op jit(solution)/shard_map/while/body/eval_jaxpr/hqk,khd->qhd/dot_general | solution.py:84
  197.8 3.0 %fusion.141 = bf16[8,512,64]{1,2,0:T(8,128)(2,1)} fusion(bf16[8,512,64]{1,2,0:T(8,128)(2,1)} %get-tuple-element.187, s32[]{:T(128)} %get-tuple-element.186, f32[512,4096]{1,0:T(8,128)S(1)} %get-tuple-element.173, f32[512]{0:T(512)S(1)} %get-tuple-element.174, s32[4096]{0:T(1024)S(1)} %get-tuple-element.200, s32[512]{0:T(512)S(1)} %dynamic_slice.21, ...), kind=kOutput, calls=%fused_computation.10.clone.1 | convolution fusion | flops 278986752 | bytes 9001472 | tf_op jit(solution)/shard_map/while/body/eval_jaxpr/hqk,khd->qhd/dot_general | solution.py:84
  202.1 2.7 fusion.139
  207.2 3.0 %fusion.141 = bf16[8,512,64]{1,2,0:T(8,128)(2,1)} fusion(bf16[8,512,64]{1,2,0:T(8,128)(2,1)} %get-tuple-element.187, s32[]{:T(128)} %get-tuple-element.186, f32[512,4096]{1,0:T(8,128)S(1)} %get-tuple-element.173, f32[512]{0:T(512)S(1)} %get-tuple-element.174, s32[4096]{0:T(1024)S(1)} %get-tuple-element.200, s32[512]{0:T(512)S(1)} %dynamic_slice.21, ...), kind=kOutput, calls=%fused_computation.10.clone.1 | convolution fusion | flops 278986752 | bytes 9001472 | tf_op jit(solution)/shard_map/while/body/eval_jaxpr/hqk,khd->qhd/dot_general | solution.py:84
  216.6 3.0 %fusion.141 = bf16[8,512,64]{1,2,0:T(8,128)(2,1)} fusion(bf16[8,512,64]{1,2,0:T(8,128)(2,1)} %get-tuple-element.187, s32[]{:T(128)} %get-tuple-element.186, f32[512,4096]{1,0:T(8,128)S(1)} %get-tuple-element.173, f32[512]{0:T(512)S(1)} %get-tuple-element.174, s32[4096]{0:T(1024)S(1)} %get-tuple-element.200, s32[512]{0:T(512)S(1)} %dynamic_slice.21, ...), kind=kOutput, calls=%fused_computation.10.clone.1 | convolution fusion | flops 278986752 | bytes 9001472 | tf_op jit(solution)/shard_map/while/body/eval_jaxpr/hqk,khd->qhd/dot_general | solution.py:84
  223.9 6.8 %all-to-all-start.1 = ((bf16[16,256,64]{1,2,0:T(8,128)(2,1)}), bf16[16,256,64]{1,2,0:T(8,128)(2,1)S(1)}, u32[]{:S(2)}, u32[]{:S(2)}) async-start(bf16[16,256,64]{1,2,0:T(8,128)(2,1)} %copy.22), calls=%async_computation.1 | async-start | bytes 1048576 | tf_op jit(solution)/shard_map/all_to_all | solution.py:95
  231.1 15.4 %all-to-all-done.1 = bf16[16,256,64]{1,2,0:T(8,128)(2,1)S(1)} async-done(((bf16[16,256,64]{1,2,0:T(8,128)(2,1)}), bf16[16,256,64]{1,2,0:T(8,128)(2,1)S(1)}, u32[]{:S(2)}, u32[]{:S(2)}) %all-to-all-start.1) | async-done | bytes 524320 | tf_op jit(solution)/shard_map/all_to_all | solution.py:95
  251.8 3.6 %collective-permute-start.2 = (bf16[15,1024]{1,0:T(8,128)(2,1)S(1)}, bf16[15,1024]{1,0:T(8,128)(2,1)S(1)}, u32[]{:S(2)}, u32[]{:S(2)}) collective-permute-start(bf16[15,1024]{1,0:T(8,128)(2,1)S(1)} %get-tuple-element.65), channel_id=1, source_target_pairs={{16,0},{32,16},{48,32},{64,48},{80,64},{96,80},{112,96},{128,112},... | collective-permute-start | bytes 92168 | tf_op jit(solution)/shard_map/ppermute | solution.py:23
  256.5 7.0 %collective-permute-start.1 = (bf16[1,15,1024]{2,1,0:T(8,128)(2,1)S(1)}, bf16[1,15,1024]{2,1,0:T(8,128)(2,1)S(1)}, u32[]{:S(2)}, u32[]{:S(2)}) collective-permute-start(bf16[1,15,1024]{2,1,0:T(8,128)(2,1)S(1)} %bitcast.127), channel_id=1, source_target_pairs={{0,1},{1,2},{2,3},{3,4},{4,5},{5,6},{6,7},{7,8},{8,9},{9,10},{10,1... | collective-permute-start | bytes 92168 | tf_op jit(solution)/shard_map/ppermute | solution.py:20
  265.6 4.8 %collective-permute-done.3 = bf16[1,15,1024]{2,1,0:T(8,128)(2,1)S(1)} collective-permute-done((bf16[1,15,1024]{2,1,0:T(8,128)(2,1)S(1)}, bf16[1,15,1024]{2,1,0:T(8,128)(2,1)S(1)}, u32[]{:S(2)}, u32[]{:S(2)}) %collective-permute-start.3) | collective-permute-done | bytes 30752 | tf_op jit(solution)/shard_map/ppermute | solution.py:23
  270.6 6.3 %fusion.122 = (f32[256]{0:T(256)S(1)}, f32[256,1024]{1,0:T(8,128)S(1)}) fusion(f32[1024]{0:T(1024)S(1)} %bitcast.139, f32[286,1024]{1,0:T(8,128)S(1)} %maximum_convert_fusion, pred[256]{0:T(512)(128)(4,1)S(1)} %get-tuple-element.98, f32[1024]{0:T(1024)S(1)} %bitcast.140, pred[256]{0:T(512)(128)(4,1)S(1)} %get-tuple-element.99, f32[1024]{0:T(1024)S(1)} %bitcast.142, ...), kind=kLoop, calls=%fused_computation.205 | loop fusion | flops 24379136 | bytes 33690368 | tf_op jit(solution)/shard_map/reduce_sum | solution.py:29
  (94 shorter events, 62.2 us)
Async XLA Ops:
  6.5 240.7 %copy-start = (bf16[1024,1024]{1,0:T(8,128)(2,1)S(1)}, bf16[1024,1024]{1,0:T(8,128)(2,1)}, u32[]{:S(2)}) copy-start(bf16[1024,1024]{1,0:T(8,128)(2,1)} %param.16) | copy-start | bytes 6291460
  6.5 76.6 %all-gather.2.cloned.1.call-start = ((), (), s32[]{:S(2)}) async-start(), calls=%async_computation.2 | async-start | bytes 6684672 | tf_op jit(solution)/shard_map/all_gather | solution.py:59
  89.2 9.5 %copy-start.8 = (s32[8]{0:T(128)S(1)}, s32[8]{0:T(128)}, u32[]{:S(2)}) copy-start(s32[8]{0:T(128)} %param.13) | copy-start | bytes 100
  91.8 43.0 %all-to-all-start = ((bf16[256,16,192]{0,2,1:T(8,128)(2,1)}), bf16[256,16,192]{0,2,1:T(8,128)(2,1)}, u32[]{:S(2)}, u32[]{:S(2)}) async-start(bf16[256,16,192]{0,2,1:T(8,128)(2,1)} %bitcast.125), calls=%async_computation | async-start | bytes 3145728 | tf_op jit(solution)/shard_map/all_to_all | solution.py:62
  219.5 11.4 %copy-start.3 = (f32[31,1024]{1,0:T(8,128)S(1)}, f32[31,1024]{1,0:T(8,128)}, u32[]{:S(2)}) copy-start(f32[31,1024]{1,0:T(8,128)} %param.19) | copy-start | bytes 380932
  219.5 27.7 %copy-start.1 = (bf16[1,256,1024]{2,1,0:T(8,128)(2,1)S(1)}, bf16[1,256,1024]{2,1,0:T(8,128)(2,1)}, u32[]{:S(2)}) copy-start(bf16[1,256,1024]{2,1,0:T(8,128)(2,1)} %param.12) | copy-start | bytes 1572868
  221.0 28.7 %copy-start.6 = (f32[1024]{0:T(1024)S(1)}, f32[1024]{0:T(1024)}, u32[]{:S(2)}) copy-start(f32[1024]{0:T(1024)} %param.17) | copy-start | bytes 12292
  223.9 22.6 %all-to-all-start.1 = ((bf16[16,256,64]{1,2,0:T(8,128)(2,1)}), bf16[16,256,64]{1,2,0:T(8,128)(2,1)S(1)}, u32[]{:S(2)}, u32[]{:S(2)}) async-start(bf16[16,256,64]{1,2,0:T(8,128)(2,1)} %copy.22), calls=%async_computation.1 | async-start | bytes 1048576 | tf_op jit(solution)/shard_map/all_to_all | solution.py:95
  246.5 0.8 copy-start.2
  247.3 2.4 copy-start.4
  251.4 5.1 %collective-permute-start = (bf16[15,1024]{1,0:T(8,128)(2,1)S(1)}, bf16[15,1024]{1,0:T(8,128)(2,1)S(1)}, u32[]{:S(2)}, u32[]{:S(2)}) collective-permute-start(bf16[15,1024]{1,0:T(8,128)(2,1)S(1)} %get-tuple-element.64), channel_id=1, source_target_pairs={{0,16},{16,32},{32,48},{48,64},{64,80},{80,96},{96,112},{112,128},... | collective-permute-start | bytes 92168 | tf_op jit(solution)/shard_map/ppermute | solution.py:20
  251.8 11.8 %collective-permute-start.2 = (bf16[15,1024]{1,0:T(8,128)(2,1)S(1)}, bf16[15,1024]{1,0:T(8,128)(2,1)S(1)}, u32[]{:S(2)}, u32[]{:S(2)}) collective-permute-start(bf16[15,1024]{1,0:T(8,128)(2,1)S(1)} %get-tuple-element.65), channel_id=1, source_target_pairs={{16,0},{32,16},{48,32},{64,48},{80,64},{96,80},{112,96},{128,112},... | collective-permute-start | bytes 92168 | tf_op jit(solution)/shard_map/ppermute | solution.py:23
  256.5 9.1 %collective-permute-start.1 = (bf16[1,15,1024]{2,1,0:T(8,128)(2,1)S(1)}, bf16[1,15,1024]{2,1,0:T(8,128)(2,1)S(1)}, u32[]{:S(2)}, u32[]{:S(2)}) collective-permute-start(bf16[1,15,1024]{2,1,0:T(8,128)(2,1)S(1)} %bitcast.127), channel_id=1, source_target_pairs={{0,1},{1,2},{2,3},{3,4},{4,5},{5,6},{6,7},{7,8},{8,9},{9,10},{10,1... | collective-permute-start | bytes 92168 | tf_op jit(solution)/shard_map/ppermute | solution.py:20
  263.7 6.7 %collective-permute-start.3 = (bf16[1,15,1024]{2,1,0:T(8,128)(2,1)S(1)}, bf16[1,15,1024]{2,1,0:T(8,128)(2,1)S(1)}, u32[]{:S(2)}, u32[]{:S(2)}) collective-permute-start(bf16[1,15,1024]{2,1,0:T(8,128)(2,1)S(1)} %bitcast.128), channel_id=1, source_target_pairs={{1,0},{2,1},{3,2},{4,3},{5,4},{6,5},{7,6},{8,7},{9,8},{10,9},{11,1... | collective-permute-start | bytes 92168 | tf_op jit(solution)/shard_map/ppermute | solution.py:23
  270.6 6.6 %copy-start.5 = (bf16[1024,1024]{1,0:T(8,128)(2,1)S(1)}, bf16[1024,1024]{1,0:T(8,128)(2,1)}, u32[]{:S(2)}) copy-start(bf16[1024,1024]{1,0:T(8,128)(2,1)} %param.21) | copy-start | bytes 6291460
  270.6 6.6 %copy-start.7 = (f32[1024]{0:T(1024)S(1)}, f32[1024]{0:T(1024)}, u32[]{:S(2)}) copy-start(f32[1024]{0:T(1024)} %param.20) | copy-start | bytes 12292
Sparse Core Ops, SparseCore 0:
  10.0 73.0 all-gather.1
where the time goes:
time: 287 us; the launch traced here: 286 us
  waiting for transfers between devices  131 us (46%)
  matrix products  55.9 us (19%)
  other arithmetic  30.3 us (11%)
  starting transfers between devices  26.6 us (9%)
  local copies, waits for them, and re-layouts  22.9 us (8%)
  between operations  13.7 us (5%)
  loops' own time  5.04 us (2%)
    all_gather x1, waiting for transfers between devices, body(): lax.all_gather(w_qkv, 'grp', axis=1, tiled=True)  73.4 us
    all_to_all x1, waiting for transfers between devices, body(): lax.all_to_all(qkv_rows, 'blk', split_axis=1, concat_axis=0, tiled=True)  35.8 us
    dot_general x8, matrix products, attend(): jnp.einsum('hqk,khd->qhd', weights.astype(jnp.bfloat16), values_all, pref...  23.7 us
    dot_general x8, matrix products, attend(): jnp.einsum('qhd,khd->hqk', queries, keys_all, preferred_element_type=jnp....  21.2 us
    reduce_sum x8, other arithmetic, attend(): row_total = jnp.sum(weights, axis=2)  19.8 us
    all_to_all x1, waiting for transfers between devices, body(): lax.all_to_all(merged_heads, 'blk', split_axis=0, concat_axis=1, tiled=True)  15.4 us
    reduce_sum x3, other arithmetic, normalize(): center = values - jnp.mean(values, axis=-1, keepdims=True)  7.59 us
    ppermute x2, starting transfers between devices, padded_2(): lax.ppermute(lax.slice_in_dim(block, block.shape[dim] - width, None, axis...  7.35 us
  transfers between devices with their start and end apart: 7, of which 5 were waited for; matrix products, arithmetic and copies ran while one was open for 1% of the time, Pallas kernels for 0%

commit v1 on v0

v1 whole, which is shorter than its diff:
```python
import functools
import math

import jax
import jax.numpy as jnp
from jax import lax
from jax.experimental import pallas as pl
from jax.experimental.pallas import tpu as pltpu
from jax.sharding import PartitionSpec as P

HEADS = 16
MESH = pl.DeviceIdType.MESH

epsilon = 1e-05
big_negative = -1e30


def normalize(values, row_gain):
    center = values - jnp.mean(values, axis=-1, keepdims=True)
    spread = jnp.mean(center * center, axis=-1, keepdims=True)
    return center * lax.rsqrt(spread + epsilon) * row_gain


def segment_of(utt_lengths, positions):
    starts = jnp.cumsum(utt_lengths) - utt_lengths
    started = (starts[None, :] <= positions[:, None]).astype(jnp.int32)
    return jnp.sum(started, axis=1) - 1


def attention_kernel(
    utt_ref, frames_ref, gain_ref, w_ref,
    att_ref,
    from_low, from_high, w_pair, stage, qkv, query, keys, scores, out_stage,
    load_sem, low_send, low_recv, high_send, high_recv, w_send, w_recv, core_send, core_recv,
    swap_send, swap_recv, out_send, out_recv,
):
    half = from_low.shape[1]
    rows = 2 * half
    blk = lax.axis_index("blk")
    grp = lax.axis_index("grp")
    z, y_low = blk // 2, blk % 2
    x, y_high, core = grp // 4, (grp // 2) % 2, grp % 2
    dx, dy = z % 4, z // 4
    w_target = ((x + 4 - dx) % 4) * 4 + ((y_high + dy) % 2) * 2 + core
    w_source = ((x + dx) % 4) * 4 + ((y_high + dy) % 2) * 2 + core
    my_head = ((x + dx) % 4) * 4 + ((y_high + dy) % 2) * 2 + y_low
    other_core = grp + 1 - 2 * core
    partner = blk + 1 - 2 * y_low
    z_up = (blk + 2) % 16
    z_down = (blk + 14) % 16

    def place(b, g):
        return {"blk": b, "grp": g}

    loads = [
        pltpu.make_async_copy(frames_ref.at[pl.ds(0, half)], from_low.at[7], load_sem.at[0]),
        pltpu.make_async_copy(frames_ref.at[pl.ds(half, half)], from_high.at[7], load_sem.at[1]),
    ]
    for load in loads:
        load.start()

    barrier = pltpu.get_barrier_semaphore()
    for step in range(1, 16):
        pl.semaphore_signal(
            barrier, inc=1, device_id=place((blk + step) % 16, grp), device_id_type=MESH
        )
    pl.semaphore_signal(barrier, inc=1, device_id=place(blk, other_core), device_id_type=MESH)

    @pl.when(z > 0)
    def _():
        pl.semaphore_signal(barrier, inc=1, device_id=place(blk, w_target), device_id_type=MESH)
        pl.semaphore_signal(barrier, inc=1, device_id=place(blk, w_source), device_id_type=MESH)

    pl.semaphore_wait(barrier, jnp.where(z > 0, 18, 16))

    def remote(src, dst, send, recv, b, g):
        return pltpu.make_async_remote_copy(
            src_ref=src, dst_ref=dst, send_sem=send, recv_sem=recv,
            device_id=place(b, g), device_id_type=MESH,
        )

    def low_copy(event, src):
        return remote(src, from_low.at[event], low_send.at[event], low_recv.at[event], z_up, grp)

    def high_copy(event, src):
        return remote(
            src, from_high.at[event], high_send.at[event], high_recv.at[event], z_down, grp
        )

    for load in loads:
        load.wait()
    low_copy(0, from_low.at[7]).start()
    high_copy(0, from_high.at[7]).start()
    low_copy(1, from_high.at[7]).start()
    high_copy(1, from_low.at[7]).start()
    w_copy = remote(w_ref, w_pair.at[core], w_send, w_recv, blk, w_target)

    @pl.when(z > 0)
    def _():
        w_copy.start()

    @pl.when(z == 0)
    def _():
        w_pair[core] = w_ref[...]

    def arrive(event):
        low_copy(event, from_low.at[event]).wait_recv()

        @pl.when(event <= 4)
        def _():
            low_copy(event + 2, from_low.at[event]).start()

        high_copy(event, from_high.at[event]).wait_recv()

        @pl.when(event <= 4)
        def _():
            high_copy(event + 2, from_high.at[event]).start()

    arrive(0)
    arrive(1)

    @pl.when(z > 0)
    def _():
        w_copy.wait_recv()

    core_copy = remote(w_pair.at[core], w_pair.at[core], core_send, core_recv, blk, other_core)
    core_copy.start()
    core_back = remote(
        w_pair.at[1 - core], w_pair.at[1 - core], core_send, core_recv, blk, other_core
    )
    core_back.wait_recv()

    scale = jnp.where(
        lax.broadcasted_iota(jnp.int32, (1, 192), 1) < 64, math.log2(math.e) / 8.0, 1.0
    )
    ones = jnp.ones((rows, 64), jnp.bfloat16)

    def sources(slot):
        own = slot == 7
        last = slot == 6
        low_z = jnp.where(own, z, jnp.where(last, z + 4, z + 7 - slot // 2)) % 8
        high_z = jnp.where(own, z, jnp.where(last, z + 4, z + 1 + slot // 2)) % 8
        odd = slot % 2
        low_half = jnp.where(own, 0, odd)
        high_half = jnp.where(own, 1, 1 - odd)
        low_row = low_z * (2 * rows) + low_half * half
        high_row = high_z * (2 * rows) + high_half * half
        return low_row, high_row

    def swap_copy(slot, side, row):
        return remote(
            stage.at[slot, side], qkv.at[pl.ds(row, half)], swap_send.at[slot, side],
            swap_recv.at[slot, side], partner, grp,
        )

    def project(index, carry):
        slot = (index + 7) % 8

        @pl.when(index >= 3)
        def _():
            arrive(index - 1)

        low_row, high_row = sources(slot)
        low_at = pl.multiple_of(low_row + y_low * rows, half)
        high_at = pl.multiple_of(high_row + y_low * rows, half)
        frames = jnp.concatenate([from_low[slot], from_high[slot]], axis=0).astype(jnp.float32)
        normed = normalize(frames, gain_ref[...]).astype(jnp.bfloat16)

        def head_rows(which):
            product = jnp.dot(normed, w_pair[which], preferred_element_type=jnp.float32) * scale
            return jnp.concatenate([product.astype(jnp.bfloat16), ones], axis=1)

        away = head_rows(1 - y_low)
        stage[slot, 0] = away[:half]
        stage[slot, 1] = away[half:]
        swap_copy(slot, 0, low_at).start()
        swap_copy(slot, 1, high_at).start()
        home = head_rows(y_low)
        qkv[pl.ds(low_at, half)] = home[:half]
        qkv[pl.ds(high_at, half)] = home[half:]
        return carry

    lax.fori_loop(0, 8, project, 0)

    lane = lax.broadcasted_iota(jnp.int32, (1, 128), 1)
    begin = jnp.zeros((1, 128), jnp.int32)
    end = jnp.zeros((1, 128), jnp.int32)
    start = jnp.int32(0)
    for c in range(8):
        stop = start + utt_ref[c]
        begin = jnp.where(lane == 64 + c, start, begin)
        end = jnp.where(lane == 64 + c, stop, end)
        start = stop

    def arrange(index, carry):
        slot = (index + 7) % 8
        low_row, high_row = sources(slot)
        for side, row in ((0, low_row), (1, high_row)):
            theirs = pl.multiple_of(row + (1 - y_low) * rows, half)
            swap_copy(slot, side, theirs).wait_recv()
            mine = pl.multiple_of(row + y_low * rows, half)
            for at in (theirs, mine):
                both = qkv[pl.ds(at, half), :128]
                position = (
                    lax.broadcasted_iota(jnp.int32, (half, 128), 0) + (at + grp * (16 * rows))
                )
                member = (position >= begin) & (position < end)
                inside = member.astype(jnp.float32)
                query_mark = jnp.where(lane < 72, (1.0 - inside) * big_negative, 0.0)
                whole = both.astype(jnp.float32)
                query[pl.ds(at, half)] = jnp.where(lane < 64, whole, query_mark).astype(
                    jnp.bfloat16
                )
                keys[pl.ds(at, half)] = jnp.where(
                    lane < 64, pltpu.roll(whole, 64, 1), inside
                ).astype(jnp.bfloat16)
        return carry

    lax.fori_loop(0, 8, arrange, 0)

    window = 16 * rows
    key_block = 512
    key_steps = window // key_block

    def score_block(block, step):
        queries = query[pl.ds(pl.multiple_of(block * rows, rows), rows)]
        return lax.dot_general(
            queries, keys[step * key_block : (step + 1) * key_block],
            (((1,), (1,)), ((), ())), preferred_element_type=jnp.float32,
        )

    def lane_max(best, block_scores):
        for piece in range(key_block // 128):
            best = jnp.maximum(best, block_scores[:, piece * 128 : (piece + 1) * 128])
        return best

    def first_pass(block, buffer):
        best = jnp.full((rows, 128), -jnp.inf, jnp.float32)
        for step in range(key_steps):
            got = score_block(block, step)
            scores[buffer, :, step * key_block : (step + 1) * key_block] = got
            best = lane_max(best, got)
        return jnp.max(best, axis=1, keepdims=True)

    def target_of(index):
        return (blk + 1 + index) % 16

    def attend(index, row_max):
        block = target_of(index)
        following = target_of(index + 1)
        buffer = index % 2
        total = jnp.zeros((rows, 128), jnp.float32)
        best = jnp.full((rows, 128), -jnp.inf, jnp.float32)
        for step in range(key_steps):
            span = slice(step * key_block, (step + 1) * key_block)
            weights = jnp.exp2(scores[buffer, :, span] - row_max).astype(jnp.bfloat16)
            got = score_block(following, step)
            scores[1 - buffer, :, span] = got
            best = lane_max(best, got)
            total = total + jnp.dot(
                weights, qkv[span, 128:], preferred_element_type=jnp.float32
            )
        mixed = total / pltpu.roll(total, 64, 1)
        packed = jnp.where(lane < 64, mixed[:half], pltpu.roll(mixed[half:], 64, 1)).astype(
            jnp.bfloat16
        )

        @pl.when(index < 15)
        def _():
            out_stage[index] = packed
            out_copy(index, block).start()

        @pl.when(index == 15)
        def _():
            att_ref[my_head] = packed

        return jnp.max(best, axis=1, keepdims=True)

    def out_copy(index, block):
        return remote(
            out_stage.at[index], att_ref.at[my_head], out_send.at[index], out_recv.at[index],
            block, grp,
        )

    lax.fori_loop(0, 16, attend, first_pass(target_of(0), 0))

    def collect(index, carry):
        from_blk = (blk + 15 - index) % 16
        from_z = from_blk // 2
        head = (
            ((x + from_z % 4) % 4) * 4 + ((y_high + from_z // 4) % 2) * 2 + from_blk % 2
        )
        got = remote(
            out_stage.at[index], att_ref.at[head], out_send.at[index], out_recv.at[index],
            from_blk, grp,
        )
        got.wait_recv()
        got.wait_send()
        return carry

    lax.fori_loop(0, 15, collect, 0)

    for event in range(7):
        low_copy(event, from_low.at[event]).wait_send()
        high_copy(event, from_high.at[event]).wait_send()
    for slot in range(8):
        for side in range(2):
            swap_copy(slot, side, 0).wait_send()
    core_copy.wait_send()

    @pl.when(z > 0)
    def _():
        w_copy.wait_send()


def attend_all(frames, utt_lengths, attn_gain, w_qkv):
    rows, width = frames.shape
    half = rows // 2
    window = rows * 16
    vmem = pl.BlockSpec(memory_space=pltpu.VMEM)
    dma = pltpu.SemaphoreType.DMA
    return pl.pallas_call(
        attention_kernel,
        out_shape=jax.ShapeDtypeStruct((HEADS, half, 128), jnp.bfloat16),
        in_specs=[
            pl.BlockSpec(memory_space=pltpu.SMEM),
            pl.BlockSpec(memory_space=pl.ANY),
            vmem,
            vmem,
        ],
        out_specs=vmem,
        scratch_shapes=[
            pltpu.VMEM((8, half, width), jnp.bfloat16),
            pltpu.VMEM((8, half, width), jnp.bfloat16),
            pltpu.VMEM((2, width, 192), jnp.bfloat16),
            pltpu.VMEM((8, 2, half, 256), jnp.bfloat16),
            pltpu.VMEM((window, 256), jnp.bfloat16),
            pltpu.VMEM((window, 128), jnp.bfloat16),
            pltpu.VMEM((window, 128), jnp.bfloat16),
            pltpu.VMEM((2, rows, window), jnp.float32),
            pltpu.VMEM((15, half, 128), jnp.bfloat16),
            dma((2,)),
            dma((7,)), dma((7,)), dma((7,)), dma((7,)),
            dma, dma, dma, dma,
            dma((8, 2)), dma((8, 2)),
            dma((15,)), dma((15,)),
        ],
        compiler_params=pltpu.CompilerParams(
            collective_id=0, has_side_effects=True, vmem_limit_bytes=48 * 1024 * 1024
        ),
    )(utt_lengths, frames, attn_gain.reshape(1, width), w_qkv)


def padded_2(block, sides, width, periodic):
    for axis, dim in sides:
        count = lax.axis_size(axis)
        forward = [(i, i + 1) for i in range(count - 1)]
        if periodic:
            forward.append((count - 1, 0))
        backward = [(target, source) for source, target in forward]
        low = lax.ppermute(
            lax.slice_in_dim(block, block.shape[dim] - width, None, axis=dim), axis, forward
        )
        high = lax.ppermute(lax.slice_in_dim(block, 0, width, axis=dim), axis, backward)
        block = jnp.concatenate([low, block, high], axis=dim)
    return block


def body(
    frames, utt_lengths, attn_gain, w_qkv, w_out, conv_gain, w_glu, w_depth, depth_gain, w_proj
):
    frame_rows = frames.shape[1]
    width = frames.shape[2]
    kernel_half = (w_depth.shape[0] - 1) // 2
    blocks = lax.axis_size("blk")
    block_index = lax.axis_index("blk")
    group_index = lax.axis_index("grp")
    window_start = group_index * frame_rows * blocks
    first_frame = window_start + block_index * frame_rows
    local_frames = frames[0]
    local_float = local_frames.astype(jnp.float32)
    local_seg = segment_of(utt_lengths, first_frame + jnp.arange(frame_rows, dtype=jnp.int32))
    packed = attend_all(local_frames, utt_lengths, attn_gain, w_qkv)
    attended = jnp.transpose(
        packed.reshape(HEADS, frame_rows // 2, 2, width // HEADS), (2, 1, 0, 3)
    ).reshape(frame_rows, width)
    residual = (local_float + jnp.dot(attended, w_out, preferred_element_type=jnp.float32)).astype(
        jnp.bfloat16
    )
    residual = lax.optimization_barrier(residual)
    conv_in = normalize(residual.astype(jnp.float32), conv_gain).astype(jnp.bfloat16)
    projected = jnp.dot(conv_in, w_glu, preferred_element_type=jnp.float32)
    gated = (projected[:, :width] * jax.nn.sigmoid(projected[:, width:])).astype(jnp.bfloat16)
    gated = lax.optimization_barrier(gated)
    padded = padded_2(gated, (("blk", 0),), kernel_half, True)
    left_rim = padded[:kernel_half]
    right_rim = padded[frame_rows + kernel_half :]
    outer_rims = padded_2(jnp.stack([right_rim, left_rim]), (("grp", 0),), 1, False)
    left_edge = jnp.where(block_index == 0, outer_rims[0], left_rim)
    right_edge = jnp.where(block_index == blocks - 1, outer_rims[3], right_rim)
    extended = jnp.concatenate([left_edge, gated, right_edge], axis=0).astype(jnp.float32)
    extended_seg = segment_of(
        utt_lengths,
        first_frame - kernel_half + jnp.arange(frame_rows + 2 * kernel_half, dtype=jnp.int32),
    )
    mixed_conv = jnp.zeros((frame_rows, width), jnp.float32)
    for offset in range(2 * kernel_half + 1):
        same_seg = (extended_seg[offset : offset + frame_rows] == local_seg)[:, None]
        mixed_conv = mixed_conv + jnp.where(
            same_seg, extended[offset : offset + frame_rows] * w_depth[offset], 0.0
        )
    normed_conv = normalize(mixed_conv, depth_gain)
    activated = (normed_conv * jax.nn.sigmoid(normed_conv)).astype(jnp.bfloat16)
    result = (
        residual.astype(jnp.float32)
        + jnp.dot(activated, w_proj, preferred_element_type=jnp.float32)
    ).astype(jnp.bfloat16)
    return result[None]


def solution(mesh):
    in_specs = (P("grp", "blk", None), P(), P(), P(None, "grp"), P(), P(), P(), P(), P(), P())
    out_specs = P("grp", "blk", None)
    return jax.shard_map(body, mesh=mesh, in_specs=in_specs, out_specs=out_specs, check_vma=False)
```

time: 287 us -> 125 us (0.44)
  waiting for transfers between devices: 131 us -> 5.29 us
  Pallas kernels: 0 us -> 88 us
  matrix products: 55.9 us -> 3.83 us
  other arithmetic: 30.3 us -> 7.97 us
  local copies, waits for them, and re-layouts: 22.9 us -> 7.48 us
  starting transfers between devices: 26.6 us -> 12.4 us
  between operations: 13.7 us -> 0.31 us
  loops' own time: 5.04 us -> 0 us
    pallas_call x0 -> x1, Pallas kernels: none -> 88 us  [attend_all(): pl.pallas_call(attention_kernel, out_shape=jax.ShapeDtypeStruct((HEADS, h...]
    all_gather x1 -> x0, waiting for transfers between devices: 73.4 us -> none  [body(): lax.all_gather(w_qkv, 'grp', axis=1, tiled=True)]
    all_to_all x2 -> x0, waiting for transfers between devices: 51.2 us -> none  [the longest x1 35.8 us: body(): lax.all_to_all(qkv_rows, 'blk', split_axis=1, concat_axis=0, tiled=True)]
    dot_general x17 -> x0, matrix products: 50.9 us -> none  [the longest x8 23.7 us: attend(): jnp.einsum('hqk,khd->qhd', weights.astype(jnp.bfloat16), values_all, pref...]
    reduce_sum x8 -> x0, other arithmetic: 19.8 us -> none  [attend(): row_total = jnp.sum(weights, axis=2)]
    all_to_all x2 -> x0, starting transfers between devices: 13.7 us -> none  [the longest x1 6.9 us: body(): lax.all_to_all(qkv_rows, 'blk', split_axis=1, concat_axis=0, tiled=True)]
    all_to_all x3 -> x0, local copies, waits for them, and re-layouts: 6.39 us -> none  [the longest x1 3.43 us: body(): lax.all_to_all(qkv_rows, 'blk', split_axis=1, concat_axis=0, tiled=True)]
    dynamic_slice x16 -> x0, local copies, waits for them, and re-layouts: 5.36 us -> none  [the longest x8 4.72 us: body(): pieces = lax.map(attend, jnp.arange(block_count, dtype=jnp.int32))]
  transfers between devices with their start and end apart: 7 -> 4, of which waited for: 5 -> 2; matrix products, arithmetic and copies ran while one was open for 1% -> 1% of each run, Pallas kernels for 0% -> 0%
where the time goes in v1:
time: 125 us
  Pallas kernels  88 us (70%)
  starting transfers between devices  12.4 us (10%)
  other arithmetic  7.97 us (6%)
  local copies, waits for them, and re-layouts  7.48 us (6%)
  waiting for transfers between devices  5.29 us (4%)
  matrix products  3.83 us (3%)
    pallas_call x1, Pallas kernels, attend_all(): pl.pallas_call(attention_kernel, out_shape=jax.ShapeDtypeStruct((HEADS, h...  88 us
    ppermute x2, starting transfers between devices, padded_2(): lax.ppermute(lax.slice_in_dim(block, block.shape[dim] - width, None, axis...  7.54 us
    reduce_sum x2, other arithmetic, normalize(): center = values - jnp.mean(values, axis=-1, keepdims=True)  6.41 us
    unnamed x25, local copies, waits for them, and re-layouts  5.52 us
    ppermute x2, starting transfers between devices, padded_2(): lax.ppermute(lax.slice_in_dim(block, 0, width, axis=dim), axis, backward)  4.85 us
    ppermute x2, waiting for transfers between devices, padded_2(): lax.ppermute(lax.slice_in_dim(block, 0, width, axis=dim), axis, backward)  4.6 us
  transfers between devices with their start and end apart: 4, of which 2 were waited for; matrix products, arithmetic and copies ran while one was open for 1% of the time, Pallas kernels for 0%

profile of v1, /device:TPU:1, one launch (start us, length us, event | category | flops | bytes accessed | tf_op | source)
XLA Modules:
  0.0 125.2 jit_solution(7931106405943318174)
XLA Ops:
  0.0 1.3 %copy.15.w_ref = bf16[1024,192]{1,0:T(8,128)(2,1)S(1)} copy(bf16[1024,192]{0,1:T(8,128)(2,1)} %param.13) | data formatting | bytes 786432 | tf_op args[3]
  1.4 1.0 copy-done.1
  2.4 0.7 copy-done.4
  3.1 0.7 copy-done.5
  3.7 88.0 %shard_map.100 = bf16[16,128,128]{2,1,0:T(8,128)(2,1)S(1)} custom-call(s32[8]{0:T(128)S(1)} %copy-done.5, bf16[256,1024]{1,0:T(8,128)(2,1)S(1)} %bitcast.58, f32[1,1024]{1,0:T(1,128)S(1)} %bitcast.59, bf16[1024,192]{1,0:T(8,128)(2,1)S(1)} %copy.15.w_ref), custom_call_target="tpu_custom_call" | custom-call | tf_op jit(solution)/shard_map/pallas_call | solution.py:322
  91.7 0.8 copy-done.3
  92.5 1.3 %copy.16 = bf16[16,128,128]{1,2,0:T(8,128)(2,1)S(1)} copy(bf16[16,128,128]{2,1,0:T(8,128)(2,1)} %copy-done.3) | data formatting | bytes 1048576 | tf_op jit(solution)/shard_map/pallas_call | solution.py:322
  93.8 0.5 copy.17
  94.4 0.7 fusion.1
  95.3 0.3 fusion.5
  95.6 1.0 copy-done.8
  96.6 1.4 %fusion.74 = f32[256,2048]{1,0:T(8,128)S(1)} fusion(bf16[1024,2048]{1,0:T(8,128)(2,1)S(1)} %copy-done.8, bf16[256,1024]{1,0:T(8,128)(2,1)S(1)} %fusion.1, f32[1024]{0:T(1024)S(1)} %copy-done.10, f32[256]{0:T(256)S(1)} %add_rsqrt_fusion.1, f32[256]{0:T(256)S(1)} %broadcast_multiply_fusion.1), kind=kOutput, calls=%fused_computation.113 | convolution fusion | flops 1075052544 | bytes 6821888 | tf_op jit(solution)/shard_map/dot_general | solution.py:392
  98.0 0.3 fusion.73
  98.3 0.9 collective-permute-start
  99.2 2.8 %collective-permute-start.2 = (bf16[15,1024]{1,0:T(8,128)(2,1)S(1)}, bf16[15,1024]{1,0:T(8,128)(2,1)S(1)}, u32[]{:S(2)}, u32[]{:S(2)}) collective-permute-start(bf16[15,1024]{1,0:T(8,128)(2,1)S(1)} %get-tuple-element.8), channel_id=1, source_target_pairs={{16,0},{32,16},{48,32},{64,48},{80,64},{96,80},{112,96},{128,112},... | collective-permute-start | bytes 92168 | tf_op jit(solution)/shard_map/ppermute | solution.py:364
  102.1 0.2 reduce-window.9
  102.6 0.7 collective-permute-done
  103.3 6.6 %collective-permute-start.1 = (bf16[1,15,1024]{2,1,0:T(8,128)(2,1)S(1)}, bf16[1,15,1024]{2,1,0:T(8,128)(2,1)S(1)}, u32[]{:S(2)}, u32[]{:S(2)}) collective-permute-start(bf16[1,15,1024]{2,1,0:T(8,128)(2,1)S(1)} %bitcast.64), channel_id=1, source_target_pairs={{0,1},{1,2},{2,3},{3,4},{4,5},{5,6},{6,7},{7,8},{8,9},{9,10},{10,1... | collective-permute-start | bytes 92168 | tf_op jit(solution)/shard_map/ppermute | solution.py:361
  110.0 2.1 %collective-permute-start.3 = (bf16[1,15,1024]{2,1,0:T(8,128)(2,1)S(1)}, bf16[1,15,1024]{2,1,0:T(8,128)(2,1)S(1)}, u32[]{:S(2)}, u32[]{:S(2)}) collective-permute-start(bf16[1,15,1024]{2,1,0:T(8,128)(2,1)S(1)} %bitcast.63), channel_id=1, source_target_pairs={{1,0},{2,1},{3,2},{4,3},{5,4},{6,5},{7,6},{8,7},{9,8},{10,9},{11,1... | collective-permute-start | bytes 92168 | tf_op jit(solution)/shard_map/ppermute | solution.py:364
  112.2 4.6 %collective-permute-done.3 = bf16[1,15,1024]{2,1,0:T(8,128)(2,1)S(1)} collective-permute-done((bf16[1,15,1024]{2,1,0:T(8,128)(2,1)S(1)}, bf16[1,15,1024]{2,1,0:T(8,128)(2,1)S(1)}, u32[]{:S(2)}, u32[]{:S(2)}) %collective-permute-start.3) | collective-permute-done | bytes 30752 | tf_op jit(solution)/shard_map/ppermute | solution.py:364
  116.8 0.2 maximum_convert_fusion
  117.0 6.3 %fusion.86 = (f32[256]{0:T(256)S(1)}, f32[256,1024]{1,0:T(8,128)S(1)}) fusion(f32[1024]{0:T(1024)S(1)} %bitcast.94, f32[286,1024]{1,0:T(8,128)S(1)} %maximum_convert_fusion, pred[256]{0:T(512)(128)(4,1)S(1)} %get-tuple-element.41, f32[1024]{0:T(1024)S(1)} %bitcast.95, pred[256]{0:T(512)(128)(4,1)S(1)} %get-tuple-element.42, f32[1024]{0:T(1024)S(1)} %bitcast.66, ...), kind=kLoop, calls=%fused_computation.168 | loop fusion | flops 24379136 | bytes 33690368 | tf_op jit(solution)/shard_map/reduce_sum | solution.py:19
  123.3 0.2 multiply_reduce_fusion
  123.5 1.7 %fusion.4 = bf16[1,256,1024]{2,1,0:T(8,128)(2,1)} fusion(bf16[1024,1024]{1,0:T(8,128)(2,1)S(1)} %copy-done.9, bf16[256,1024]{1,0:T(8,128)(2,1)S(1)} %fusion.1, f32[256,1024]{1,0:T(8,128)S(1)} %get-tuple-element.6, f32[1024]{0:T(1024)S(1)} %copy-done.11, f32[256]{0:T(256)S(1)} %add_rsqrt_fusion, f32[256]{0:T(256)S(1)} %broadcast_multiply_fusion), kind=kOutput, calls=%fused_computation.8 | convolution fusion | flops 539754496 | bytes 4200448 | tf_op jit(solution)/shard_map/dot_general | solution.py:416
  (39 shorter events, 0.7 us)
Async XLA Ops:
  0.0 94.4 %copy-start = (bf16[1024,1024]{1,0:T(8,128)(2,1)S(1)}, bf16[1024,1024]{1,0:T(8,128)(2,1)}, u32[]{:S(2)}) copy-start(bf16[1024,1024]{1,0:T(8,128)(2,1)} %param.14) | copy-start | bytes 6291460
  0.0 94.4 %copy-start.2 = (bf16[1,256,1024]{2,1,0:T(8,128)(2,1)S(1)}, bf16[1,256,1024]{2,1,0:T(8,128)(2,1)}, u32[]{:S(2)}) copy-start(bf16[1,256,1024]{2,1,0:T(8,128)(2,1)} %param.10) | copy-start | bytes 1572868
  1.4 1.0 copy-start.1
  2.4 0.7 copy-start.4
  3.1 0.7 copy-start.5
  91.7 0.8 copy-start.3
  94.4 2.2 %copy-start.8 = (bf16[1024,2048]{1,0:T(8,128)(2,1)S(1)}, bf16[1024,2048]{1,0:T(8,128)(2,1)}, u32[]{:S(2)}) copy-start(bf16[1024,2048]{1,0:T(8,128)(2,1)} %param.16) | copy-start | bytes 12582916
  94.4 2.2 %copy-start.10 = (f32[1024]{0:T(1024)S(1)}, f32[1024]{0:T(1024)}, u32[]{:S(2)}) copy-start(f32[1024]{0:T(1024)} %param.15) | copy-start | bytes 12292
  98.0 4.0 %copy-start.7 = (f32[31,1024]{1,0:T(8,128)S(1)}, f32[31,1024]{1,0:T(8,128)}, u32[]{:S(2)}) copy-start(f32[31,1024]{1,0:T(8,128)} %param.17) | copy-start | bytes 380932
  98.0 4.1 %copy-start.6 = (s32[8]{0:T(128)S(1)}, s32[8]{0:T(128)}, u32[]{:S(2)}) copy-start(s32[8]{0:T(128)} %utt_ref.1) | copy-start | bytes 100
  98.3 5.0 %collective-permute-start = (bf16[15,1024]{1,0:T(8,128)(2,1)S(1)}, bf16[15,1024]{1,0:T(8,128)(2,1)S(1)}, u32[]{:S(2)}, u32[]{:S(2)}) collective-permute-start(bf16[15,1024]{1,0:T(8,128)(2,1)S(1)} %get-tuple-element.7), channel_id=1, source_target_pairs={{0,16},{16,32},{32,48},{48,64},{64,80},{80,96},{96,112},{112,128},... | collective-permute-start | bytes 92168 | tf_op jit(solution)/shard_map/ppermute | solution.py:361
  99.2 10.8 %collective-permute-start.2 = (bf16[15,1024]{1,0:T(8,128)(2,1)S(1)}, bf16[15,1024]{1,0:T(8,128)(2,1)S(1)}, u32[]{:S(2)}, u32[]{:S(2)}) collective-permute-start(bf16[15,1024]{1,0:T(8,128)(2,1)S(1)} %get-tuple-element.8), channel_id=1, source_target_pairs={{16,0},{32,16},{48,32},{64,48},{80,64},{96,80},{112,96},{128,112},... | collective-permute-start | bytes 92168 | tf_op jit(solution)/shard_map/ppermute | solution.py:364
  103.3 8.9 %collective-permute-start.1 = (bf16[1,15,1024]{2,1,0:T(8,128)(2,1)S(1)}, bf16[1,15,1024]{2,1,0:T(8,128)(2,1)S(1)}, u32[]{:S(2)}, u32[]{:S(2)}) collective-permute-start(bf16[1,15,1024]{2,1,0:T(8,128)(2,1)S(1)} %bitcast.64), channel_id=1, source_target_pairs={{0,1},{1,2},{2,3},{3,4},{4,5},{5,6},{6,7},{7,8},{8,9},{9,10},{10,1... | collective-permute-start | bytes 92168 | tf_op jit(solution)/shard_map/ppermute | solution.py:361
  110.0 6.7 %collective-permute-start.3 = (bf16[1,15,1024]{2,1,0:T(8,128)(2,1)S(1)}, bf16[1,15,1024]{2,1,0:T(8,128)(2,1)S(1)}, u32[]{:S(2)}, u32[]{:S(2)}) collective-permute-start(bf16[1,15,1024]{2,1,0:T(8,128)(2,1)S(1)} %bitcast.63), channel_id=1, source_target_pairs={{1,0},{2,1},{3,2},{4,3},{5,4},{6,5},{7,6},{8,7},{9,8},{10,9},{11,1... | collective-permute-start | bytes 92168 | tf_op jit(solution)/shard_map/ppermute | solution.py:364
  117.0 6.6 %copy-start.9 = (bf16[1024,1024]{1,0:T(8,128)(2,1)S(1)}, bf16[1024,1024]{1,0:T(8,128)(2,1)}, u32[]{:S(2)}) copy-start(bf16[1024,1024]{1,0:T(8,128)(2,1)} %param.19) | copy-start | bytes 6291460
  117.0 6.6 %copy-start.11 = (f32[1024]{0:T(1024)S(1)}, f32[1024]{0:T(1024)}, u32[]{:S(2)}) copy-start(f32[1024]{0:T(1024)} %param.18) | copy-start | bytes 12292

commit v2 on v0

v2 whole, which is shorter than its diff:
```python
import functools
import math

import jax
import jax.numpy as jnp
from jax import lax
from jax.experimental import pallas as pl
from jax.experimental.pallas import tpu as pltpu
from jax.sharding import PartitionSpec as P

HEADS = 16
SETS = 8
HALO = 16
MESH = pl.DeviceIdType.MESH

epsilon = 1e-05
big_negative = -1e30
lowest = -2e38


def normalize(values, row_gain):
    center = values - jnp.mean(values, axis=-1, keepdims=True)
    spread = jnp.mean(center * center, axis=-1, keepdims=True)
    return center * lax.rsqrt(spread + epsilon) * row_gain


def mixing_kernel(
    utt_hbm, frames_hbm, gain_hbm, w_hbm, w_out_hbm, conv_gain_hbm, w_glu_hbm,
    gated_ref, residual_ref,
    utt, gain, conv_gain, w_mine, w_out, w_glu,
    from_low, from_high, w_pair, stage, qkv, query, keys, peak, mix, buf_a, buf_b,
    out_stage, att, attended,
    load_sem, low_send, low_recv, high_send, high_recv, w_send, w_recv, core_send, core_recv,
    swap_send, swap_recv, out_send, out_recv, halo_send, halo_recv,
):
    half = from_low.shape[1]
    rows = 2 * half
    blk = lax.axis_index("blk")
    grp = lax.axis_index("grp")
    z, y_low = blk // 2, blk % 2
    x, y_high, core = grp // 4, (grp // 2) % 2, grp % 2
    dx, dy = z % 4, z // 4
    head_x, head_y = (x + dx) % 4, (y_high + dy) % 2
    w_source = head_x * 4 + head_y * 2 + core
    w_target = ((x + 4 - dx) % 4) * 4 + head_y * 2 + core
    my_head = head_x * 4 + head_y * 2 + y_low
    other_core = grp + 1 - 2 * core
    partner = blk + 1 - 2 * y_low
    z_up = (blk + 2) % 16
    z_down = (blk + 14) % 16
    left = ((blk + 15) % 16, (grp + jnp.where(blk == 0, 15, 0)) % 16)
    right = ((blk + 1) % 16, (grp + jnp.where(blk == 15, 1, 0)) % 16)

    def place(b, g):
        return {"blk": b, "grp": g}

    def load(index, src, dst):
        return pltpu.make_async_copy(src, dst, load_sem.at[index])

    loads = [
        load(0, frames_hbm.at[pl.ds(0, half)], from_low.at[7]),
        load(1, frames_hbm.at[pl.ds(half, half)], from_high.at[7]),
        load(2, w_hbm, w_mine),
        load(3, gain_hbm, gain),
        load(4, utt_hbm, utt),
        load(5, conv_gain_hbm, conv_gain),
        load(6, w_out_hbm, w_out),
        load(7, w_glu_hbm, w_glu),
    ]
    for item in loads:
        item.start()

    barrier = pltpu.get_barrier_semaphore()

    def greet(b, g):
        pl.semaphore_signal(barrier, inc=1, device_id=place(b, g), device_id_type=MESH)

    for step in range(1, 16):
        greet((blk + step) % 16, grp)
    greet(blk, other_core)
    greet(*left)
    greet(*right)

    @pl.when(z > 0)
    def _():
        greet(blk, w_target)
        greet(blk, w_source)

    pl.semaphore_wait(barrier, jnp.where(z > 0, 20, 18))

    def remote(src, dst, send, recv, b, g):
        return pltpu.make_async_remote_copy(
            src_ref=src, dst_ref=dst, send_sem=send, recv_sem=recv,
            device_id=place(b, g), device_id_type=MESH,
        )

    def low_copy(event, src):
        return remote(src, from_low.at[event], low_send.at[event], low_recv.at[event], z_up, grp)

    def high_copy(event, src):
        return remote(
            src, from_high.at[event], high_send.at[event], high_recv.at[event], z_down, grp
        )

    loads[0].wait()
    loads[1].wait()
    low_copy(0, from_low.at[7]).start()
    high_copy(0, from_high.at[7]).start()
    low_copy(1, from_high.at[7]).start()
    high_copy(1, from_low.at[7]).start()
    loads[2].wait()
    w_copy = remote(w_mine, w_pair.at[core], w_send, w_recv, blk, w_target)

    @pl.when(z > 0)
    def _():
        w_copy.start()

    @pl.when(z == 0)
    def _():
        w_pair[core] = w_mine[...]

    loads[3].wait()
    loads[4].wait()

    def arrive(event):
        low_copy(event, from_low.at[event]).wait_recv()

        @pl.when(event <= 4)
        def _():
            low_copy(event + 2, from_low.at[event]).start()

        high_copy(event, from_high.at[event]).wait_recv()

        @pl.when(event <= 4)
        def _():
            high_copy(event + 2, from_high.at[event]).start()

    arrive(0)
    arrive(1)

    @pl.when(z > 0)
    def _():
        w_copy.wait_recv()

    core_copy = remote(w_pair.at[core], w_pair.at[core], core_send, core_recv, blk, other_core)
    core_copy.start()
    core_back = remote(
        w_pair.at[1 - core], w_pair.at[1 - core], core_send, core_recv, blk, other_core
    )
    core_back.wait_recv()

    lane = lax.broadcasted_iota(jnp.int32, (1, 128), 1)
    begin = jnp.zeros((1, 128), jnp.int32)
    end = jnp.zeros((1, 128), jnp.int32)
    start = jnp.int32(0)
    for c in range(8):
        stop = start + utt[c]
        begin = jnp.where(lane == 64 + c, start, begin)
        end = jnp.where(lane == 64 + c, stop, end)
        start = stop
    scale = jnp.where(
        lax.broadcasted_iota(jnp.int32, (1, 192), 1) < 64, math.log2(math.e) / 8.0, 1.0
    )
    ones = jnp.ones((rows, 64), jnp.bfloat16)

    def chunk_of(s, side):
        event = s + 7
        odd = event % 2
        away = jnp.where(s == 0, 0, jnp.where(s == 7, 4, (s + 1) // 2))
        if side == 0:
            return (z + 8 - away) % 8, jnp.where(s == 0, 0, odd)
        return (z + away) % 8, jnp.where(s == 0, 1, 1 - odd)

    def swap_copy(s, side):
        return remote(
            stage.at[s, side], qkv.at[s, pl.ds(rows + side * half, half)],
            swap_send.at[s, side], swap_recv.at[s, side], partner, grp,
        )

    def project(s):
        slot = (s + 7) % 8
        frames = jnp.concatenate([from_low[slot], from_high[slot]], axis=0).astype(jnp.float32)
        normed = normalize(frames, gain[...]).astype(jnp.bfloat16)

        def head_rows(which):
            product = lax.dot_general(
                normed, w_pair[which], (((1,), (1,)), ((), ())),
                preferred_element_type=jnp.float32,
            ) * scale
            return jnp.concatenate([product.astype(jnp.bfloat16), ones], axis=1)

        theirs = head_rows(1 - y_low)
        stage[s, 0] = theirs[:half]
        stage[s, 1] = theirs[half:]
        swap_copy(s, 0).start()
        swap_copy(s, 1).start()
        qkv[s, :rows] = head_rows(y_low)

    def arrange(s):
        swap_copy(s, 0).wait_recv()
        swap_copy(s, 1).wait_recv()
        for piece in range(4):
            from_z, from_half = chunk_of(s, piece % 2)
            plane = y_low if piece < 2 else 1 - y_low
            first = grp * (16 * rows) + (from_z * 2 + plane) * rows + from_half * half
            span = slice(piece * half, (piece + 1) * half)
            whole = qkv[s, span, :128].astype(jnp.float32)
            position = lax.broadcasted_iota(jnp.int32, (half, 128), 0) + first
            inside = ((position >= begin) & (position < end)).astype(jnp.float32)
            query_mark = jnp.where(lane < 72, (1.0 - inside) * big_negative, 0.0)
            query[s, span] = jnp.where(lane < 64, whole, query_mark).astype(jnp.bfloat16)
            keys[s, span] = jnp.where(lane < 64, pltpu.roll(whole, 64, 1), inside).astype(
                jnp.bfloat16
            )
        peak[s] = jnp.full((2 * rows, 128), lowest, jnp.float32)
        mix[s] = jnp.zeros((2 * rows, 128), jnp.float32)

    def score(q, k):
        return lax.dot_general(
            query[q], keys[k], (((1,), (1,)), ((), ())), preferred_element_type=jnp.float32
        )

    def absorb(q, k, buf):
        tiles = [buf[:, t * 128 : (t + 1) * 128] for t in range(2 * rows // 128)]
        old = peak[q]
        new = jnp.maximum(
            old, jnp.max(functools.reduce(jnp.maximum, tiles), axis=1, keepdims=True)
        )
        weights = jnp.concatenate(
            [jnp.exp2(tile - new).astype(jnp.bfloat16) for tile in tiles], axis=1
        )
        mix[q] = mix[q] * jnp.exp2(old - new) + jnp.dot(
            weights, qkv[k, :, 128:], preferred_element_type=jnp.float32
        )
        peak[q] = new

    def pair(s, p):
        return jnp.where(p <= s, s, 2 * s - p), jnp.where(p <= s, p, s)

    def two_pairs(s, t):
        q0, k0 = pair(s, 2 * t)
        q1, k1 = pair(s, 2 * t + 1)
        q2, k2 = pair(s, 2 * t + 2)
        buf_b[...] = score(q1, k1)
        absorb(q0, k0, buf_a)
        buf_a[...] = score(q2, k2)
        absorb(q1, k1, buf_b)
        return q0, q1

    def first_score(s):
        buf_a[...] = score(s, 0)

    def attend(s):
        first_score(s)

        def both(t, carry):
            two_pairs(s, t)
            return carry

        lax.fori_loop(0, s, both, 0)
        absorb(*pair(s, 2 * s), buf_a)

    def step(s, carry):
        @pl.when(s >= 3)
        def _():
            arrive(s - 1)

        project(s)

        @pl.when(s >= 1)
        def _():
            arrange(s - 1)
            attend(s - 1)

        return carry

    lax.fori_loop(0, SETS, step, 0)

    def out_copy(s, piece):
        to_z, to_half = chunk_of(s, piece % 2)
        plane = y_low if piece < 2 else 1 - y_low
        return remote(
            out_stage.at[s, piece], att.at[my_head, to_half], out_send.at[s, piece],
            out_recv.at[s, piece], to_z * 2 + plane, grp,
        )

    def finish(s):
        total = mix[s]
        mixed = total / pltpu.roll(total, 64, 1)
        turned = pltpu.roll(mixed, 64, 1)
        quarter = half // 2
        packed = [
            jnp.where(
                lane < 64, mixed[piece * half : piece * half + quarter],
                turned[piece * half + quarter : (piece + 1) * half],
            ).astype(jnp.bfloat16)
            for piece in range(4)
        ]

        @pl.when(s > 0)
        def _():
            for piece in range(2):
                out_stage[s, piece] = packed[piece]
                out_copy(s, piece).start()

        @pl.when(s == 0)
        def _():
            att[my_head, 0] = packed[0]
            att[my_head, 1] = packed[1]

        for piece in range(2, 4):
            out_stage[s, piece] = packed[piece]
            out_copy(s, piece).start()

    last = SETS - 1
    arrange(last)
    first_score(last)

    def gather_last(t, carry):
        two_pairs(last, t)
        return carry

    lax.fori_loop(0, 4, gather_last, 0)
    finish(last)

    def release(t, carry):
        q0, q1 = two_pairs(last, t)
        finish(q0)
        finish(q1)
        return carry

    lax.fori_loop(4, 7, release, 0)
    absorb(*pair(last, 2 * last), buf_a)
    finish(0)
    loads[5].wait()
    loads[6].wait()
    loads[7].wait()

    def collect(s, carry):
        for piece in range(4):
            plane = y_low if piece < 2 else 1 - y_low
            from_z, _ = chunk_of(s, 1 - piece % 2)
            _, at_half = chunk_of(s, piece % 2)
            head = ((x + from_z % 4) % 4) * 4 + ((y_high + from_z // 4) % 2) * 2 + plane
            got = remote(
                out_stage.at[s, piece], att.at[head, at_half], out_send.at[s, piece],
                out_recv.at[s, piece], from_z * 2 + plane, grp,
            )
            if piece < 2:
                @pl.when(s > 0)
                def _():
                    got.wait_recv()
                    got.wait_send()
            else:
                got.wait_recv()
                got.wait_send()
        return carry

    lax.fori_loop(0, SETS, collect, 0)

    quarter = half // 2
    for side in range(2):
        for two in range(HEADS // 2):
            one = att[2 * two, side].astype(jnp.float32)
            other = att[2 * two + 1, side].astype(jnp.float32)
            top = jnp.where(lane < 64, one, pltpu.roll(other, 64, 1))
            low = jnp.where(lane < 64, pltpu.roll(one, 64, 1), other)
            span = slice(two * 128, (two + 1) * 128)
            at = side * half
            attended[at : at + quarter, span] = top.astype(jnp.bfloat16)
            attended[at + quarter : at + half, span] = low.astype(jnp.bfloat16)

    frames = jnp.concatenate([from_low[7], from_high[7]], axis=0).astype(jnp.float32)
    residual = (
        frames + jnp.dot(attended[...], w_out[...], preferred_element_type=jnp.float32)
    ).astype(jnp.bfloat16)
    residual_ref[...] = residual
    conv_in = normalize(residual.astype(jnp.float32), conv_gain[...]).astype(jnp.bfloat16)
    width = residual.shape[1]
    for column in range(0, width, 256):
        values = jnp.dot(
            conv_in, w_glu[:, column : column + 256], preferred_element_type=jnp.float32
        )
        gates = jnp.dot(
            conv_in, w_glu[:, width + column : width + column + 256],
            preferred_element_type=jnp.float32,
        )
        gated_ref[HALO : HALO + rows, column : column + 256] = (
            values * jax.nn.sigmoid(gates)
        ).astype(jnp.bfloat16)

    to_left = remote(
        gated_ref.at[pl.ds(HALO, HALO)], gated_ref.at[pl.ds(HALO + rows, HALO)],
        halo_send.at[0], halo_recv.at[0], *left,
    )
    to_right = remote(
        gated_ref.at[pl.ds(rows, HALO)], gated_ref.at[pl.ds(0, HALO)],
        halo_send.at[1], halo_recv.at[1], *right,
    )
    to_left.start()
    to_right.start()

    for event in range(7):
        low_copy(event, from_low.at[event]).wait_send()
        high_copy(event, from_high.at[event]).wait_send()
    for s in range(SETS):
        for side in range(2):
            swap_copy(s, side).wait_send()
    core_copy.wait_send()

    @pl.when(z > 0)
    def _():
        w_copy.wait_send()

    to_left.wait()
    to_right.wait()


def mix_all(frames, utt_lengths, attn_gain, w_qkv, w_out, conv_gain, w_glu):
    rows, width = frames.shape
    half = rows // 2
    hbm = pl.BlockSpec(memory_space=pltpu.HBM)
    vmem = pl.BlockSpec(memory_space=pltpu.VMEM)
    dma = pltpu.SemaphoreType.DMA
    bf16, f32 = jnp.bfloat16, jnp.float32
    return pl.pallas_call(
        mixing_kernel,
        out_shape=(
            jax.ShapeDtypeStruct((rows + 2 * HALO, width), bf16),
            jax.ShapeDtypeStruct((rows, width), bf16),
        ),
        in_specs=[hbm] * 7,
        out_specs=(vmem, vmem),
        scratch_shapes=[
            pltpu.SMEM((8,), jnp.int32),
            pltpu.VMEM((1, width), f32),
            pltpu.VMEM((1, width), f32),
            pltpu.VMEM((192, width), bf16),
            pltpu.VMEM((width, width), bf16),
            pltpu.VMEM((width, 2 * width), bf16),
            pltpu.VMEM((8, half, width), bf16),
            pltpu.VMEM((8, half, width), bf16),
            pltpu.VMEM((2, 192, width), bf16),
            pltpu.VMEM((SETS, 2, half, 256), bf16),
            pltpu.VMEM((SETS, 2 * rows, 256), bf16),
            pltpu.VMEM((SETS, 2 * rows, 128), bf16),
            pltpu.VMEM((SETS, 2 * rows, 128), bf16),
            pltpu.VMEM((SETS, 2 * rows, 128), f32),
            pltpu.VMEM((SETS, 2 * rows, 128), f32),
            pltpu.VMEM((2 * rows, 2 * rows), f32),
            pltpu.VMEM((2 * rows, 2 * rows), f32),
            pltpu.VMEM((SETS, 4, half // 2, 128), bf16),
            pltpu.VMEM((HEADS, 2, half // 2, 128), bf16),
            pltpu.VMEM((rows, width), bf16),
            dma((8,)),
            dma((7,)), dma((7,)), dma((7,)), dma((7,)),
            dma, dma, dma, dma,
            dma((SETS, 2)), dma((SETS, 2)),
            dma((SETS, 4)), dma((SETS, 4)),
            dma((2,)), dma((2,)),
        ],
        compiler_params=pltpu.CompilerParams(
            collective_id=0, has_side_effects=True, vmem_limit_bytes=44 * 1024 * 1024
        ),
    )(
        utt_lengths, frames, attn_gain.reshape(1, width), w_qkv.T, w_out,
        conv_gain.reshape(1, width), w_glu,
    )


def conv_kernel(
    utt, gated_ref, residual_ref, w_depth_ref, gain_ref, w_proj_ref,
    out_ref,
    tall, mixed, activated,
):
    rows, width = residual_ref.shape
    taps = w_depth_ref.shape[0]
    reach = taps // 2
    columns = width // 128
    first = (lax.axis_index("grp") * 16 + lax.axis_index("blk")) * rows
    for c in range(columns):
        tall[c] = gated_ref[:, c * 128 : (c + 1) * 128].astype(jnp.float32)

    block = 64

    def convolve(r, carry):
        base = pl.multiple_of(r * block, block)
        position = first + base
        start = jnp.int32(0)
        low, high = jnp.int32(0), jnp.int32(0)
        for c in range(8):
            stop = start + utt[c]
            low = jnp.where(start <= position, start, low)
            high = jnp.where(start <= position, stop, high)
            start = stop
        whole = (low <= position - reach) & (high >= position + block + reach)

        def taps_of(mask):
            def column(c, carry):
                total = jnp.zeros((block, 128), jnp.float32)
                for t in range(taps):
                    term = (
                        tall[c, pl.ds(base + (HALO - reach + t), block)]
                        * w_depth_ref[t : t + 1, pl.ds(pl.multiple_of(c * 128, 128), 128)]
                    )
                    if mask is not None:
                        term = mask(t, term)
                    total = total + term
                mixed[c, pl.ds(base, block)] = total
                return carry

            lax.fori_loop(0, columns, column, 0)

        @pl.when(whole)
        def _():
            taps_of(None)

        @pl.when(jnp.logical_not(whole))
        def _():
            at = lax.broadcasted_iota(jnp.int32, (block, 128), 0) + position
            begin = jnp.zeros((block, 128), jnp.int32)
            end = jnp.zeros((block, 128), jnp.int32)
            start = jnp.int32(0)
            for c in range(8):
                stop = start + utt[c]
                begin = jnp.where(at >= start, start, begin)
                end = jnp.where(at >= start, stop, end)
                start = stop
            first_tap = begin - at + reach
            last_tap = end - at + reach
            taps_of(lambda t, term: jnp.where((first_tap <= t) & (last_tap > t), term, 0.0))

        pieces = [mixed[c, pl.ds(base, block)] for c in range(columns)]
        mean = jnp.sum(functools.reduce(jnp.add, pieces), axis=1, keepdims=True) / width
        pieces = [piece - mean for piece in pieces]
        spread = (
            jnp.sum(functools.reduce(jnp.add, [p * p for p in pieces]), axis=1, keepdims=True)
            / width
        )
        factor = lax.rsqrt(spread + epsilon)
        for c in range(columns):
            span = slice(c * 128, (c + 1) * 128)
            value = pieces[c] * factor * gain_ref[:, span]
            activated[pl.ds(base, block), span] = (value * jax.nn.sigmoid(value)).astype(
                jnp.bfloat16
            )
        return carry

    lax.fori_loop(0, rows // block, convolve, 0)
    for column in range(0, width, 256):
        span = slice(column, column + 256)
        out_ref[:, span] = (
            residual_ref[:, span].astype(jnp.float32)
            + jnp.dot(activated[...], w_proj_ref[:, span], preferred_element_type=jnp.float32)
        ).astype(jnp.bfloat16)


def convolve_all(utt_lengths, gated, residual, w_depth, depth_gain, w_proj):
    rows, width = residual.shape
    vmem = pl.BlockSpec(memory_space=pltpu.VMEM)
    return pl.pallas_call(
        conv_kernel,
        out_shape=jax.ShapeDtypeStruct((rows, width), jnp.bfloat16),
        in_specs=[pl.BlockSpec(memory_space=pltpu.SMEM)] + [vmem] * 5,
        out_specs=vmem,
        scratch_shapes=[
            pltpu.VMEM((width // 128, rows + 2 * HALO, 128), jnp.float32),
            pltpu.VMEM((width // 128, rows, 128), jnp.float32),
            pltpu.VMEM((rows, width), jnp.bfloat16),
        ],
        compiler_params=pltpu.CompilerParams(vmem_limit_bytes=24 * 1024 * 1024),
    )(utt_lengths, gated, residual, w_depth, depth_gain.reshape(1, width), w_proj)


def body(
    frames, utt_lengths, attn_gain, w_qkv, w_out, conv_gain, w_glu, w_depth, depth_gain, w_proj
):
    gated, residual = mix_all(
        frames[0], utt_lengths, attn_gain, w_qkv, w_out, conv_gain, w_glu
    )
    return convolve_all(utt_lengths, gated, residual, w_depth, depth_gain, w_proj)[None]


def solution(mesh):
    in_specs = (P("grp", "blk", None), P(), P(), P(None, "grp"), P(), P(), P(), P(), P(), P())
    out_specs = P("grp", "blk", None)
    return jax.shard_map(body, mesh=mesh, in_specs=in_specs, out_specs=out_specs, check_vma=False)
```

time: 287 us -> 103 us (0.36)
  waiting for transfers between devices: 131 us -> 0 us
  Pallas kernels: 0 us -> 94.4 us
  matrix products: 55.9 us -> 0 us
  other arithmetic: 30.3 us -> 0 us
  starting transfers between devices: 26.6 us -> 0 us
  local copies, waits for them, and re-layouts: 22.9 us -> 7.85 us
  between operations: 13.7 us -> 0.04 us
  loops' own time: 5.04 us -> 0 us
    pallas_call x0 -> x2, Pallas kernels: none -> 94.4 us  [the longest x1 88.5 us: mix_all(): pl.pallas_call(mixing_kernel, out_shape=(jax.ShapeDtypeStruct((rows + 2 *...]
    all_gather x1 -> x0, waiting for transfers between devices: 73.4 us -> none  [body(): lax.all_gather(w_qkv, 'grp', axis=1, tiled=True)]
    dot_general x20 -> x0, matrix products: 55.9 us -> none  [the longest x8 23.7 us: attend(): jnp.einsum('hqk,khd->qhd', weights.astype(jnp.bfloat16), values_all, pref...]
    all_to_all x2 -> x0, waiting for transfers between devices: 51.2 us -> none  [the longest x1 35.8 us: body(): lax.all_to_all(qkv_rows, 'blk', split_axis=1, concat_axis=0, tiled=True)]
    reduce_sum x17 -> x0, other arithmetic: 29.5 us -> none  [the longest x8 19.8 us: attend(): row_total = jnp.sum(weights, axis=2)]
    all_to_all x2 -> x0, starting transfers between devices: 13.7 us -> none  [the longest x1 6.9 us: body(): lax.all_to_all(qkv_rows, 'blk', split_axis=1, concat_axis=0, tiled=True)]
    ppermute x4 -> x0, starting transfers between devices: 12.8 us -> none  [the longest x2 7.35 us: padded_2(): lax.ppermute(lax.slice_in_dim(block, block.shape[dim] - width, None, axis...]
    unnamed x18 -> x20, local copies, waits for them, and re-layouts: 0.83 us -> 7.85 us
  transfers between devices with their start and end apart: 7 -> 0, of which waited for: 5 -> 0; matrix products, arithmetic and copies ran while one was open for 1% -> 0% of each run, Pallas kernels for 0% -> 0%
where the time goes in v2:
time: 103 us; the launch traced here: 102 us
  Pallas kernels  94.4 us (92%)
  local copies, waits for them, and re-layouts  7.85 us (8%)
    pallas_call x1, Pallas kernels, mix_all(): pl.pallas_call(mixing_kernel, out_shape=(jax.ShapeDtypeStruct((rows + 2 *...  88.5 us
    unnamed x20, local copies, waits for them, and re-layouts  7.85 us
    pallas_call x1, Pallas kernels, convolve_all(): pl.pallas_call(conv_kernel, out_shape=jax.ShapeDtypeStruct((rows, width),...  5.93 us

profile of v2, /device:TPU:1, one launch (start us, length us, event | category | flops | bytes accessed | tf_op | source)
XLA Modules:
  0.0 102.3 jit_solution(11863019184707071264)
XLA Ops:
  0.0 0.0 copy-start
  0.0 2.2 %copy-done = bf16[1024,2048]{1,0:T(8,128)(2,1)S(1)} copy-done((bf16[1024,2048]{1,0:T(8,128)(2,1)S(1)}, bf16[1024,2048]{1,0:T(8,128)(2,1)}, u32[]{:S(2)}) %copy-start) | copy-done | bytes 4194328
  2.2 0.0 copy-start.1
  2.2 1.6 %copy-done.1 = bf16[1024,1024]{1,0:T(8,128)(2,1)S(1)} copy-done((bf16[1024,1024]{1,0:T(8,128)(2,1)S(1)}, bf16[1024,1024]{1,0:T(8,128)(2,1)}, u32[]{:S(2)}) %copy-start.1) | copy-done | bytes 2097176
  3.8 0.0 copy-start.3
  3.8 1.0 %copy-done.3 = bf16[1,256,1024]{2,1,0:T(8,128)(2,1)S(1)} copy-done((bf16[1,256,1024]{2,1,0:T(8,128)(2,1)S(1)}, bf16[1,256,1024]{2,1,0:T(8,128)(2,1)}, u32[]{:S(2)}) %copy-start.3) | copy-done | bytes 524312
  4.8 0.0 copy-start.4
  4.8 1.0 copy-done.4
  5.8 0.0 copy-start.6
  5.8 0.7 copy-done.6
  6.5 0.0 copy-start.7
  6.5 0.7 copy-done.7
  7.2 0.0 copy-start.9
  7.2 0.7 copy-done.9
  7.8 0.0 copy-start.2
  7.9 0.0 copy-start.5
  7.9 0.0 copy-start.8
  7.9 88.5 %shard_map.100 = (bf16[288,1024]{1,0:T(8,128)(2,1)S(1)}, bf16[256,1024]{1,0:T(8,128)(2,1)S(1)}) custom-call(s32[8]{0:T(128)S(1)} %copy-done.9, bf16[256,1024]{1,0:T(8,128)(2,1)S(1)} %bitcast.6, f32[1,1024]{1,0:T(1,128)S(1)} %bitcast.8, bf16[192,1024]{1,0:T(8,128)(2,1)S(1)} %bitcast.7, bf16[1024,1024]{1,0:T(8,128)(2,1)S(1)} %copy-done.1, ...), custom_call_target="tpu_custom_call" | custom-call | tf_op jit(solution)/shard_map/pallas_call | solution.py:426
  96.3 0.0 copy-done.2
  96.3 0.0 copy-done.5
  96.4 0.0 copy-done.8
  96.4 5.9 %shard_map.101 = bf16[256,1024]{1,0:T(8,128)(2,1)} custom-call(s32[8]{0:T(128)S(1)} %copy-done.9, bf16[288,1024]{1,0:T(8,128)(2,1)S(1)} %get-tuple-element.7.gated_ref, bf16[256,1024]{1,0:T(8,128)(2,1)S(1)} %get-tuple-element.8.residual_ref, f32[31,1024]{1,0:T(8,128)S(1)} %copy-done.5, f32[1,1024]{1,0:T(1,128)S(1)} %bitcast.10, bf16[1024,1024]{1,0:T(8,128)(2,1)S(1)} %copy-done.2), custom_call_target="tpu_custom_call" | custom-call | tf_op jit(solution)/shard_map/pallas_call | solution.py:561
Async XLA Ops:
  0.0 2.2 %copy-start = (bf16[1024,2048]{1,0:T(8,128)(2,1)S(1)}, bf16[1024,2048]{1,0:T(8,128)(2,1)}, u32[]{:S(2)}) copy-start(bf16[1024,2048]{1,0:T(8,128)(2,1)} %w_glu_hbm.1) | copy-start | bytes 12582916
  2.2 1.6 %copy-start.1 = (bf16[1024,1024]{1,0:T(8,128)(2,1)S(1)}, bf16[1024,1024]{1,0:T(8,128)(2,1)}, u32[]{:S(2)}) copy-start(bf16[1024,1024]{1,0:T(8,128)(2,1)} %w_out_hbm.1) | copy-start | bytes 6291460
  3.8 1.0 %copy-start.3 = (bf16[1,256,1024]{2,1,0:T(8,128)(2,1)S(1)}, bf16[1,256,1024]{2,1,0:T(8,128)(2,1)}, u32[]{:S(2)}) copy-start(bf16[1,256,1024]{2,1,0:T(8,128)(2,1)} %param.10) | copy-start | bytes 1572868
  4.8 1.0 copy-start.4
  5.8 0.7 copy-start.6
  6.5 0.7 copy-start.7
  7.2 0.7 copy-start.9
  7.8 88.5 %copy-start.2 = (bf16[1024,1024]{1,0:T(8,128)(2,1)S(1)}, bf16[1024,1024]{1,0:T(8,128)(2,1)}, u32[]{:S(2)}) copy-start(bf16[1024,1024]{1,0:T(8,128)(2,1)} %w_proj_ref.1) | copy-start | bytes 6291460
  7.9 88.5 %copy-start.5 = (f32[31,1024]{1,0:T(8,128)S(1)}, f32[31,1024]{1,0:T(8,128)}, u32[]{:S(2)}) copy-start(f32[31,1024]{1,0:T(8,128)} %w_depth_ref.1) | copy-start | bytes 380932
  7.9 88.5 %copy-start.8 = (f32[1024]{0:T(1024)S(1)}, f32[1024]{0:T(1024)}, u32[]{:S(2)}) copy-start(f32[1024]{0:T(1024)} %param.18) | copy-start | bytes 12292

commit v3 on v2

--- a/solution.py
+++ b/solution.py
@@ -25,11 +25,12 @@
 
 
 def mixing_kernel(
-    utt_hbm, frames_hbm, gain_hbm, w_hbm, w_out_hbm, conv_gain_hbm, w_glu_hbm,
-    gated_ref, residual_ref,
-    utt, gain, conv_gain, w_mine, w_out, w_glu,
+    utt_hbm, frames_hbm, gain_hbm, w_hbm, w_out_hbm, conv_gain_hbm, w_glu_hbm, w_depth_hbm,
+    depth_gain_hbm, w_proj_hbm,
+    out_ref,
+    utt, gain, conv_gain, depth_gain, w_mine, w_out, w_glu, w_depth, w_proj,
     from_low, from_high, w_pair, stage, qkv, query, keys, peak, mix, buf_a, buf_b,
-    out_stage, att, attended,
+    out_stage, att, attended, residual, edge_out, edge_in, tall, valid, mixed,
     load_sem, low_send, low_recv, high_send, high_recv, w_send, w_recv, core_send, core_recv,
     swap_send, swap_recv, out_send, out_recv, halo_send, halo_recv,
 ):
@@ -66,6 +67,9 @@
         load(5, conv_gain_hbm, conv_gain),
         load(6, w_out_hbm, w_out),
         load(7, w_glu_hbm, w_glu),
+        load(8, w_depth_hbm, w_depth),
+        load(9, depth_gain_hbm, depth_gain),
+        load(10, w_proj_hbm, w_proj),
     ]
     for item in loads:
         item.start()
@@ -237,24 +241,21 @@
     def pair(s, p):
         return jnp.where(p <= s, s, 2 * s - p), jnp.where(p <= s, p, s)
 
-    def two_pairs(s, t):
-        q0, k0 = pair(s, 2 * t)
-        q1, k1 = pair(s, 2 * t + 1)
-        q2, k2 = pair(s, 2 * t + 2)
+    def two_pairs(order, s, t):
+        q0, k0 = order(s, 2 * t)
+        q1, k1 = order(s, 2 * t + 1)
+        q2, k2 = order(s, 2 * t + 2)
         buf_b[...] = score(q1, k1)
         absorb(q0, k0, buf_a)
         buf_a[...] = score(q2, k2)
         absorb(q1, k1, buf_b)
         return q0, q1
 
-    def first_score(s):
+    def attend(s):
         buf_a[...] = score(s, 0)
 
-    def attend(s):
-        first_score(s)
-
         def both(t, carry):
-            two_pairs(s, t)
+            two_pairs(pair, s, t)
             return carry
 
         lax.fori_loop(0, s, both, 0)
@@ -313,28 +314,34 @@
             out_copy(s, piece).start()
 
     last = SETS - 1
+
+    def last_pair(s, p):
+        return jnp.where(p < s, s - 1 - p, s), jnp.where(p < s, s, p - s)
+
     arrange(last)
-    first_score(last)
-
-    def gather_last(t, carry):
-        two_pairs(last, t)
+    buf_a[...] = score(*last_pair(last, 0))
+
+    def release(t, carry):
+        q0, q1 = two_pairs(last_pair, last, t)
+        finish(q0)
+
+        @pl.when(t < 3)
+        def _():
+            finish(q1)
+
         return carry
 
-    lax.fori_loop(0, 4, gather_last, 0)
+    lax.fori_loop(0, 4, release, 0)
+
+    def own_last(t, carry):
+        two_pairs(last_pair, last, t)
+        return carry
+
+    lax.fori_loop(4, 7, own_last, 0)
+    absorb(*last_pair(last, 2 * last), buf_a)
     finish(last)
-
-    def release(t, carry):
-        q0, q1 = two_pairs(last, t)
-        finish(q0)
-        finish(q1)
-        return carry
-
-    lax.fori_loop(4, 7, release, 0)
-    absorb(*pair(last, 2 * last), buf_a)
-    finish(0)
-    loads[5].wait()
-    loads[6].wait()
-    loads[7].wait()
+    for item in loads[5:]:
+        item.wait()
 
     def collect(s, carry):
         for piece in range(4):
@@ -371,12 +378,13 @@
             attended[at + quarter : at + half, span] = low.astype(jnp.bfloat16)
 
     frames = jnp.concatenate([from_low[7], from_high[7]], axis=0).astype(jnp.float32)
-    residual = (
+    added = (
         frames + jnp.dot(attended[...], w_out[...], preferred_element_type=jnp.float32)
     ).astype(jnp.bfloat16)
-    residual_ref[...] = residual
-    conv_in = normalize(residual.astype(jnp.float32), conv_gain[...]).astype(jnp.bfloat16)
-    width = residual.shape[1]
+    residual[...] = added
+    conv_in = normalize(added.astype(jnp.float32), conv_gain[...]).astype(jnp.bfloat16)
+    width = added.shape[1]
+    columns = width // 128
     for column in range(0, width, 256):
         values = jnp.dot(
             conv_in, w_glu[:, column : column + 256], preferred_element_type=jnp.float32
@@ -385,20 +393,84 @@
             conv_in, w_glu[:, width + column : width + column + 256],
             preferred_element_type=jnp.float32,
         )
-        gated_ref[HALO : HALO + rows, column : column + 256] = (
-            values * jax.nn.sigmoid(gates)
-        ).astype(jnp.bfloat16)
-
-    to_left = remote(
-        gated_ref.at[pl.ds(HALO, HALO)], gated_ref.at[pl.ds(HALO + rows, HALO)],
-        halo_send.at[0], halo_recv.at[0], *left,
-    )
-    to_right = remote(
-        gated_ref.at[pl.ds(rows, HALO)], gated_ref.at[pl.ds(0, HALO)],
-        halo_send.at[1], halo_recv.at[1], *right,
-    )
+        gated = (values * jax.nn.sigmoid(gates)).astype(jnp.bfloat16)
+        edge_out[0, :, column : column + 256] = gated[:HALO]
+        edge_out[1, :, column : column + 256] = gated[rows - HALO :]
+        wide = gated.astype(jnp.float32)
+        for c in range(2):
+            tall[column // 128 + c, HALO : HALO + rows] = wide[:, c * 128 : (c + 1) * 128]
+
+    to_left = remote(edge_out.at[0], edge_in.at[1], halo_send.at[0], halo_recv.at[0], *left)
+    to_right = remote(edge_out.at[1], edge_in.at[0], halo_send.at[1], halo_recv.at[1], *right)
     to_left.start()
     to_right.start()
+
+    taps = w_depth.shape[0]
+    reach = taps // 2
+    block = 64
+    first_frame = (grp * 16 + blk) * rows
+
+    def convolve(base):
+        at = lax.broadcasted_iota(jnp.int32, (block, 128), 0) + (first_frame + base)
+        first = jnp.zeros((block, 128), jnp.int32)
+        final = jnp.zeros((block, 128), jnp.int32)
+        begun = jnp.int32(0)
+        for c in range(8):
+            over = begun + utt[c]
+            first = jnp.where(at >= begun, begun, first)
+            final = jnp.where(at >= begun, over, final)
+            begun = over
+        first_tap = first - at + reach
+        last_tap = final - at + reach
+        for t in range(taps):
+            valid[t] = jnp.where((first_tap <= t) & (last_tap > t), 1.0, 0.0)
+
+        def column_of(c, carry):
+            total = jnp.zeros((block, 128), jnp.float32)
+            for t in range(taps):
+                total = total + (
+                    tall[c, pl.ds(base + (HALO - reach + t), block)] * valid[t]
+                    * w_depth[t : t + 1, pl.ds(pl.multiple_of(c * 128, 128), 128)]
+                )
+            mixed[c] = total
+            return carry
+
+        lax.fori_loop(0, columns, column_of, 0)
+        pieces = [mixed[c] for c in range(columns)]
+        mean = jnp.sum(functools.reduce(jnp.add, pieces), axis=1, keepdims=True) / width
+        pieces = [piece - mean for piece in pieces]
+        spread = (
+            jnp.sum(functools.reduce(jnp.add, [p * p for p in pieces]), axis=1, keepdims=True)
+            / width
+        )
+        factor = lax.rsqrt(spread + epsilon)
+        for c in range(columns):
+            span = slice(c * 128, (c + 1) * 128)
+            value = pieces[c] * factor * depth_gain[:, span]
+            attended[pl.ds(base, block), span] = (value * jax.nn.sigmoid(value)).astype(
+                jnp.bfloat16
+            )
+
+    def conv_step(index, carry):
+        @pl.when(index == rows // block - 2)
+        def _():
+            to_left.wait_recv()
+            to_right.wait_recv()
+            for c in range(columns):
+                span = slice(c * 128, (c + 1) * 128)
+                tall[c, :HALO] = edge_in[0, :, span].astype(jnp.float32)
+                tall[c, HALO + rows :] = edge_in[1, :, span].astype(jnp.float32)
+
+        convolve(pl.multiple_of((index + 1) % (rows // block) * block, block))
+        return carry
+
+    lax.fori_loop(0, rows // block, conv_step, 0)
+    for column in range(0, width, 256):
+        span = slice(column, column + 256)
+        out_ref[:, span] = (
+            residual[:, span].astype(jnp.float32)
+            + jnp.dot(attended[...], w_proj[:, span], preferred_element_type=jnp.float32)
+        ).astype(jnp.bfloat16)
 
     for event in range(7):
         low_copy(event, from_low.at[event]).wait_send()
@@ -412,32 +484,35 @@
     def _():
         w_copy.wait_send()
 
-    to_left.wait()
-    to_right.wait()
-
-
-def mix_all(frames, utt_lengths, attn_gain, w_qkv, w_out, conv_gain, w_glu):
+    to_left.wait_send()
+    to_right.wait_send()
+
+
+def block_of(
+    frames, utt_lengths, attn_gain, w_qkv, w_out, conv_gain, w_glu, w_depth, depth_gain, w_proj
+):
     rows, width = frames.shape
     half = rows // 2
+    columns = width // 128
+    taps = w_depth.shape[0]
     hbm = pl.BlockSpec(memory_space=pltpu.HBM)
-    vmem = pl.BlockSpec(memory_space=pltpu.VMEM)
     dma = pltpu.SemaphoreType.DMA
     bf16, f32 = jnp.bfloat16, jnp.float32
     return pl.pallas_call(
         mixing_kernel,
-        out_shape=(
-            jax.ShapeDtypeStruct((rows + 2 * HALO, width), bf16),
-            jax.ShapeDtypeStruct((rows, width), bf16),
-        ),
-        in_specs=[hbm] * 7,
-        out_specs=(vmem, vmem),
+        out_shape=jax.ShapeDtypeStruct((rows, width), bf16),
+        in_specs=[hbm] * 10,
+        out_specs=pl.BlockSpec(memory_space=pltpu.VMEM),
         scratch_shapes=[
             pltpu.SMEM((8,), jnp.int32),
+            pltpu.VMEM((1, width), f32),
             pltpu.VMEM((1, width), f32),
             pltpu.VMEM((1, width), f32),
             pltpu.VMEM((192, width), bf16),
             pltpu.VMEM((width, width), bf16),
             pltpu.VMEM((width, 2 * width), bf16),
+            pltpu.VMEM((taps, width), f32),
+            pltpu.VMEM((width, width), bf16),
             pltpu.VMEM((8, half, width), bf16),
             pltpu.VMEM((8, half, width), bf16),
             pltpu.VMEM((2, 192, width), bf16),
@@ -452,7 +527,13 @@
             pltpu.VMEM((SETS, 4, half // 2, 128), bf16),
             pltpu.VMEM((HEADS, 2, half // 2, 128), bf16),
             pltpu.VMEM((rows, width), bf16),
-            dma((8,)),
+            pltpu.VMEM((rows, width), bf16),
+            pltpu.VMEM((2, HALO, width), bf16),
+            pltpu.VMEM((2, HALO, width), bf16),
+            pltpu.VMEM((columns, rows + 2 * HALO, 128), f32),
+            pltpu.VMEM((taps, 64, 128), f32),
+            pltpu.VMEM((columns, 64, 128), f32),
+            dma((11,)),
             dma((7,)), dma((7,)), dma((7,)), dma((7,)),
             dma, dma, dma, dma,
             dma((SETS, 2)), dma((SETS, 2)),
@@ -460,125 +541,16 @@
             dma((2,)), dma((2,)),
         ],
         compiler_params=pltpu.CompilerParams(
-            collective_id=0, has_side_effects=True, vmem_limit_bytes=44 * 1024 * 1024
+            collective_id=0, has_side_effects=True, vmem_limit_bytes=67043328
         ),
     )(
         utt_lengths, frames, attn_gain.reshape(1, width), w_qkv.T, w_out,
-        conv_gain.reshape(1, width), w_glu,
+        conv_gain.reshape(1, width), w_glu, w_depth, depth_gain.reshape(1, width), w_proj,
     )
 
 
-def conv_kernel(
-    utt, gated_ref, residual_ref, w_depth_ref, gain_ref, w_proj_ref,
-    out_ref,
-    tall, mixed, activated,
-):
-    rows, width = residual_ref.shape
-    taps = w_depth_ref.shape[0]
-    reach = taps // 2
-    columns = width // 128
-    first = (lax.axis_index("grp") * 16 + lax.axis_index("blk")) * rows
-    for c in range(columns):
-        tall[c] = gated_ref[:, c * 128 : (c + 1) * 128].astype(jnp.float32)
-
-    block = 64
-
-    def convolve(r, carry):
-        base = pl.multiple_of(r * block, block)
-        position = first + base
-        start = jnp.int32(0)
-        low, high = jnp.int32(0), jnp.int32(0)
-        for c in range(8):
-            stop = start + utt[c]
-            low = jnp.where(start <= position, start, low)
-            high = jnp.where(start <= position, stop, high)
-            start = stop
-        whole = (low <= position - reach) & (high >= position + block + reach)
-
-        def taps_of(mask):
-            def column(c, carry):
-                total = jnp.zeros((block, 128), jnp.float32)
-                for t in range(taps):
-                    term = (
-                        tall[c, pl.ds(base + (HALO - reach + t), block)]
-                        * w_depth_ref[t : t + 1, pl.ds(pl.multiple_of(c * 128, 128), 128)]
-                    )
-                    if mask is not None:
-                        term = mask(t, term)
-                    total = total + term
-                mixed[c, pl.ds(base, block)] = total
-                return carry
-
-            lax.fori_loop(0, columns, column, 0)
-
-        @pl.when(whole)
-        def _():
-            taps_of(None)
-
-        @pl.when(jnp.logical_not(whole))
-        def _():
-            at = lax.broadcasted_iota(jnp.int32, (block, 128), 0) + position
-            begin = jnp.zeros((block, 128), jnp.int32)
-            end = jnp.zeros((block, 128), jnp.int32)
-            start = jnp.int32(0)
-            for c in range(8):
-                stop = start + utt[c]
-                begin = jnp.where(at >= start, start, begin)
-                end = jnp.where(at >= start, stop, end)
-                start = stop
-            first_tap = begin - at + reach
-            last_tap = end - at + reach
-            taps_of(lambda t, term: jnp.where((first_tap <= t) & (last_tap > t), term, 0.0))
-
-        pieces = [mixed[c, pl.ds(base, block)] for c in range(columns)]
-        mean = jnp.sum(functools.reduce(jnp.add, pieces), axis=1, keepdims=True) / width
-        pieces = [piece - mean for piece in pieces]
-        spread = (
-            jnp.sum(functools.reduce(jnp.add, [p * p for p in pieces]), axis=1, keepdims=True)
-            / width
-        )
-        factor = lax.rsqrt(spread + epsilon)
-        for c in range(columns):
-            span = slice(c * 128, (c + 1) * 128)
-            value = pieces[c] * factor * gain_ref[:, span]
-            activated[pl.ds(base, block), span] = (value * jax.nn.sigmoid(value)).astype(
-                jnp.bfloat16
-            )
-        return carry
-
-    lax.fori_loop(0, rows // block, convolve, 0)
-    for column in range(0, width, 256):
-        span = slice(column, column + 256)
-        out_ref[:, span] = (
-            residual_ref[:, span].astype(jnp.float32)
-            + jnp.dot(activated[...], w_proj_ref[:, span], preferred_element_type=jnp.float32)
-        ).astype(jnp.bfloat16)
-
-
-def convolve_all(utt_lengths, gated, residual, w_depth, depth_gain, w_proj):
-    rows, width = residual.shape
-    vmem = pl.BlockSpec(memory_space=pltpu.VMEM)
-    return pl.pallas_call(
-        conv_kernel,
-        out_shape=jax.ShapeDtypeStruct((rows, width), jnp.bfloat16),
-        in_specs=[pl.BlockSpec(memory_space=pltpu.SMEM)] + [vmem] * 5,
-        out_specs=vmem,
-        scratch_shapes=[
-            pltpu.VMEM((width // 128, rows + 2 * HALO, 128), jnp.float32),
-            pltpu.VMEM((width // 128, rows, 128), jnp.float32),
-            pltpu.VMEM((rows, width), jnp.bfloat16),
-        ],
-        compiler_params=pltpu.CompilerParams(vmem_limit_bytes=24 * 1024 * 1024),
-    )(utt_lengths, gated, residual, w_depth, depth_gain.reshape(1, width), w_proj)
-
-
-def body(
-    frames, utt_lengths, attn_gain, w_qkv, w_out, conv_gain, w_glu, w_depth, depth_gain, w_proj
-):
-    gated, residual = mix_all(
-        frames[0], utt_lengths, attn_gain, w_qkv, w_out, conv_gain, w_glu
-    )
-    return convolve_all(utt_lengths, gated, residual, w_depth, depth_gain, w_proj)[None]
+def body(frames, *others):
+    return block_of(frames[0], *others)[None]
 
 
 def solution(mesh):

time: 103 us -> 92.3 us (0.90)
  local copies, waits for them, and re-layouts: 7.85 us -> 1.87 us
  Pallas kernels: 94.4 us -> 90.3 us
    unnamed x20 -> x1, local copies, waits for them, and re-layouts: 7.85 us -> 1.87 us
    pallas_call x2 -> x1, Pallas kernels: 94.4 us -> 90.3 us  [block_of(): pl.pallas_call(mixing_kernel, out_shape=jax.ShapeDtypeStruct((rows, width...]
where the time goes in v3:
time: 92.3 us; the launch traced here: 92.2 us
  Pallas kernels  90.3 us (98%)
  local copies, waits for them, and re-layouts  1.87 us (2%)
    pallas_call x1, Pallas kernels, block_of(): pl.pallas_call(mixing_kernel, out_shape=jax.ShapeDtypeStruct((rows, width...  90.3 us
    unnamed x1, local copies, waits for them, and re-layouts  1.87 us

profile of v3, /device:TPU:1, one launch (start us, length us, event | category | flops | bytes accessed | tf_op | source)
XLA Modules:
  0.0 92.2 jit_solution(197207085837864421)
XLA Ops:
  0.0 90.3 %shard_map.100 = bf16[256,1024]{1,0:T(8,128)(2,1)} custom-call(s32[8]{0:T(128)} %utt_hbm.1, bf16[256,1024]{1,0:T(8,128)(2,1)} %bitcast.7, f32[1,1024]{1,0:T(1,128)} %bitcast.9, bf16[192,1024]{1,0:T(8,128)(2,1)} %bitcast.8, bf16[1024,1024]{1,0:T(8,128)(2,1)} %w_out_hbm.1, f32[1,1024]{1,0:T(1,128)} %bitcast.10, bf16[1024,2048]{1,0:T(8,128)(2,1)} %w_glu_hbm.1, ...), custom_call_target="tpu_custom_call" | custom-call | tf_op jit(solution)/shard_map/pallas_call | solution.py:501
  90.3 1.9 %copy.12 = bf16[1,256,1024]{2,1,0:T(8,128)(2,1)} copy(bf16[1,256,1024]{2,1,0:T(8,128)(2,1)} %bitcast.6) | data formatting | bytes 1048576

commit v4 on v3

v4 whole, which is shorter than its diff:
```python
import functools
import math

import jax
import jax.numpy as jnp
from jax import lax
from jax.experimental import pallas as pl
from jax.experimental.pallas import tpu as pltpu
from jax.sharding import PartitionSpec as P

SETS = 8
NEAR = 4
HALO = 16
MESH = pl.DeviceIdType.MESH

epsilon = 1e-05
big_negative = -1e30
lowest = -2e38


def normalize(values, row_gain):
    center = values - jnp.mean(values, axis=-1, keepdims=True)
    spread = jnp.mean(center * center, axis=-1, keepdims=True)
    return center * lax.rsqrt(spread + epsilon) * row_gain


def mixing_kernel(
    utt_hbm, frames_hbm, gain_hbm, w_hbm, w_out_hbm, conv_gain_hbm, w_glu_hbm, w_depth_hbm,
    depth_gain_hbm, w_proj_hbm,
    out_ref,
    utt, gain, conv_gain, depth_gain, w_mine, w_out, w_glu, w_depth, w_proj,
    from_low, from_high, w_kv, w_q, kv_stage, q_stage, kv_land, q_land, query, keys, vals,
    peak, mix, buf_a, buf_b, out_stage, attended, activated, residual, edge_out, edge_in, tall, valid, mixed,
    load_sem, low_send, low_recv, high_send, high_recv, w_send, w_recv, core_send, core_recv,
    kv_send, kv_recv, q_send, q_recv, out_send, out_recv, halo_send, halo_recv,
):
    half = from_low.shape[1]
    rows = 2 * half
    blk = lax.axis_index("blk")
    grp = lax.axis_index("grp")
    z, y_low = blk // 2, blk % 2
    x, y_high, core = grp // 4, (grp // 2) % 2, grp % 2
    quad = z % 4

    def member(of_quad, m):
        odd = of_quad % 2
        return jnp.where(odd == 1, of_quad, 2 * m), jnp.where(odd == 1, m, of_quad // 2)

    def head_of(of_quad, m, of_core):
        right_by, across = member(of_quad, m)
        return ((x + right_by) % 4) * 4 + ((y_high + across) % 2) * 2 + of_core

    other_core = grp + 1 - 2 * core
    partner = blk + 1 - 2 * y_low

    def w_from(m):
        return jnp.where(member(quad, m)[1] == 1, partner, blk), head_of(quad, m, core)

    def w_to(m):
        right_by, across = member(quad, m)
        return (
            jnp.where(across == 1, partner, blk),
            ((x + 4 - right_by) % 4) * 4 + ((y_high + across) % 2) * 2 + core,
        )

    def unless_own(m, act):
        if m == 1:
            act()
        else:
            pl.when(quad > 0)(act)
    z_up = (blk + 2) % 16
    z_down = (blk + 14) % 16
    left = ((blk + 15) % 16, (grp + jnp.where(blk == 0, 15, 0)) % 16)
    right = ((blk + 1) % 16, (grp + jnp.where(blk == 15, 1, 0)) % 16)

    def place(b, g):
        return {"blk": b, "grp": g}

    def load(index, src, dst):
        return pltpu.make_async_copy(src, dst, load_sem.at[index])

    loads = [
        load(0, frames_hbm.at[pl.ds(0, half)], from_low.at[7]),
        load(1, frames_hbm.at[pl.ds(half, half)], from_high.at[7]),
        load(2, w_hbm, w_mine),
        load(3, gain_hbm, gain),
        load(4, utt_hbm, utt),
        load(5, conv_gain_hbm, conv_gain),
        load(7, w_glu_hbm, w_glu),
        load(8, w_depth_hbm, w_depth),
        load(9, depth_gain_hbm, depth_gain),
        load(6, w_proj_hbm, w_proj),
    ]
    for slot in range(SETS):
        for m in range(2):
            head = head_of(slot // 2, m, slot % 2)
            loads.append(
                load(
                    10 + 2 * slot + m,
                    w_out_hbm.at[pl.ds(pl.multiple_of(head * 64, 64), 64)],
                    w_out.at[pl.ds(slot * 128 + m * 64, 64)],
                )
            )
    for item in loads:
        item.start()

    barrier = pltpu.get_barrier_semaphore()

    def greet(b, g):
        pl.semaphore_signal(barrier, inc=1, device_id=place(b, g), device_id_type=MESH)

    for step in range(1, 16):
        greet((blk + step) % 16, grp)
    greet(blk, other_core)
    greet(*left)
    greet(*right)

    for m in range(2):
        def greet_both(m=m):
            greet(*w_to(m))
            greet(*w_from(m))

        unless_own(m, greet_both)

    pl.semaphore_wait(barrier, jnp.where(quad > 0, 22, 20))

    def remote(src, dst, send, recv, b, g):
        return pltpu.make_async_remote_copy(
            src_ref=src, dst_ref=dst, send_sem=send, recv_sem=recv,
            device_id=place(b, g), device_id_type=MESH,
        )

    def low_copy(event, src):
        return remote(src, from_low.at[event], low_send.at[event], low_recv.at[event], z_up, grp)

    def high_copy(event, src):
        return remote(
            src, from_high.at[event], high_send.at[event], high_recv.at[event], z_down, grp
        )

    loads[0].wait()
    loads[1].wait()
    low_copy(0, from_low.at[7]).start()
    high_copy(0, from_high.at[7]).start()
    low_copy(1, from_high.at[7]).start()
    high_copy(1, from_low.at[7]).start()
    loads[2].wait()

    def w_copies(m):
        return (
            remote(
                w_mine.at[pl.ds(64, 128)], w_kv.at[core, pl.ds(m * 128, 128)],
                w_send.at[m, 0], w_recv.at[m, 0], *w_to(m),
            ),
            remote(
                w_mine.at[pl.ds(0, 64)], w_q.at[core, pl.ds(m * 64, 64)],
                w_send.at[m, 1], w_recv.at[m, 1], *w_to(m),
            ),
        )

    def start_w(m):
        for item in w_copies(m):
            item.start()

    for m in range(2):
        unless_own(m, functools.partial(start_w, m))

    @pl.when(quad == 0)
    def _():
        w_kv[core, :128] = w_mine[64:]
        w_q[core, :64] = w_mine[:64]

    loads[3].wait()
    loads[4].wait()

    def arrive(event):
        low_copy(event, from_low.at[event]).wait_recv()

        @pl.when(event <= 4)
        def _():
            low_copy(event + 2, from_low.at[event]).start()

        high_copy(event, from_high.at[event]).wait_recv()

        @pl.when(event <= 4)
        def _():
            high_copy(event + 2, from_high.at[event]).start()

    arrive(0)
    arrive(1)

    def await_w(m):
        for item in w_copies(m):
            item.wait_recv()

    for m in range(2):
        unless_own(m, functools.partial(await_w, m))

    def core_copies(which):
        return (
            remote(
                w_kv.at[which], w_kv.at[which], core_send.at[0], core_recv.at[0], blk, other_core
            ),
            remote(w_q.at[which], w_q.at[which], core_send.at[1], core_recv.at[1], blk, other_core),
        )

    for item in core_copies(core):
        item.start()
    for item in core_copies(1 - core):
        item.wait_recv()

    lane = lax.broadcasted_iota(jnp.int32, (1, 128), 1)
    begin = jnp.zeros((1, 128), jnp.int32)
    end = jnp.zeros((1, 128), jnp.int32)
    start = jnp.int32(0)
    for c in range(8):
        stop = start + utt[c]
        begin = jnp.where(lane == 64 + c, start, begin)
        end = jnp.where(lane == 64 + c, stop, end)
        start = stop
    scale = math.log2(math.e) / 8.0

    def chunk_of(s, side):
        event = s + 7
        odd = event % 2
        away = jnp.where(s == 0, 0, jnp.where(s == 7, 4, (s + 1) // 2))
        if side == 0:
            return (z + 8 - away) % 8, jnp.where(s == 0, 0, odd)
        return (z + away) % 8, jnp.where(s == 0, 1, 1 - odd)

    def kv_copy(s):
        return remote(
            kv_stage.at[s], kv_land.at[s, pl.ds(rows, rows)], kv_send.at[s], kv_recv.at[s],
            partner, grp,
        )

    def q_copy(s):
        return remote(
            q_stage.at[s], q_land.at[s, pl.ds(rows, rows)], q_send.at[s], q_recv.at[s],
            partner, grp,
        )

    def times(values, weights):
        return lax.dot_general(
            values, weights, (((1,), (1,)), ((), ())), preferred_element_type=jnp.float32
        )

    def project(s):
        slot = (s + 7) % 8
        frames = jnp.concatenate([from_low[slot], from_high[slot]], axis=0).astype(jnp.float32)
        normed = normalize(frames, gain[...]).astype(jnp.bfloat16)
        kv_stage[s] = times(normed, w_kv[1 - y_low]).astype(jnp.bfloat16)
        kv_copy(s).start()

        @pl.when(s < NEAR)
        def _():
            q_stage[s] = (times(normed, w_q[1 - y_low]) * scale).astype(jnp.bfloat16)
            q_copy(s).start()
            q_land[s, :rows] = (times(normed, w_q[y_low]) * scale).astype(jnp.bfloat16)

        kv_land[s, :rows] = times(normed, w_kv[y_low]).astype(jnp.bfloat16)

    def marks(s, piece):
        from_z, from_half = chunk_of(s, piece % 2)
        plane = y_low if piece < 2 else 1 - y_low
        first = grp * (16 * rows) + (from_z * 2 + plane) * rows + from_half * half
        position = lax.broadcasted_iota(jnp.int32, (half, 128), 0) + first
        return ((position >= begin) & (position < end)).astype(jnp.float32)

    def arrange(s):
        kv_copy(s).wait_recv()
        for piece in range(4):
            span = slice(piece * half, (piece + 1) * half)
            inside = marks(s, piece)
            for m in range(2):
                both = kv_land[s, span, m * 128 : (m + 1) * 128].astype(jnp.float32)
                keys[m, s, span] = jnp.where(lane < 64, both, inside).astype(jnp.bfloat16)
                vals[m, s, span] = jnp.where(lane < 64, 1.0, both).astype(jnp.bfloat16)

        @pl.when(s < NEAR)
        def _():
            q_copy(s).wait_recv()
            for piece in range(4):
                span = slice(piece * half, (piece + 1) * half)
                outside = jnp.where(lane < 72, (1.0 - marks(s, piece)) * big_negative, 0.0)
                both = q_land[s, span].astype(jnp.float32)
                query[0, s, span] = jnp.where(lane < 64, both, outside).astype(jnp.bfloat16)
                query[1, s, span] = jnp.where(lane < 64, pltpu.roll(both, 64, 1), outside).astype(
                    jnp.bfloat16
                )
            for m in range(2):
                peak[m, s] = jnp.full((2 * rows, 128), lowest, jnp.float32)
                mix[m, s] = jnp.zeros((2 * rows, 128), jnp.float32)

    def score(m, q, k):
        return times(query[m, q], keys[m, k])

    def absorb(m, q, k, buf):
        tiles = [buf[:, t * 128 : (t + 1) * 128] for t in range(2 * rows // 128)]
        old = peak[m, q]
        new = jnp.maximum(
            old, jnp.max(functools.reduce(jnp.maximum, tiles), axis=1, keepdims=True)
        )
        weights = jnp.concatenate(
            [jnp.exp2(tile - new).astype(jnp.bfloat16) for tile in tiles], axis=1
        )
        mix[m, q] = mix[m, q] * jnp.exp2(old - new) + jnp.dot(
            weights, vals[m, k], preferred_element_type=jnp.float32
        )
        peak[m, q] = new

    def pair(s, p):
        near = s < NEAR
        return (
            jnp.where(near, jnp.where(p <= s, s, p - s - 1), NEAR - 1 - p),
            jnp.where(near & (p <= s), p, s),
        )

    def both_heads(s, p):
        q, k = pair(s, p)
        buf_b[...] = score(1, q, k)
        absorb(0, q, k, buf_a)
        buf_a[...] = score(0, *pair(s, p + 1))
        absorb(1, q, k, buf_b)

    def last_heads(s, p):
        q, k = pair(s, p)
        buf_b[...] = score(1, q, k)
        absorb(0, q, k, buf_a)
        absorb(1, q, k, buf_b)

    def attend(s):
        count = jnp.where(s < NEAR, 2 * s + 1, NEAR)
        buf_a[...] = score(0, *pair(s, 0))

        def one(p, carry):
            both_heads(s, p)
            return carry

        lax.fori_loop(0, count - 1, one, 0)
        last_heads(s, count - 1)

    def step(s, carry):
        @pl.when(s >= 3)
        def _():
            arrive(s - 1)

        project(s)

        @pl.when(s >= 1)
        def _():
            arrange(s - 1)
            attend(s - 1)

        return carry

    lax.fori_loop(0, SETS, step, 0)

    slot_of_mine = quad * 2 + y_low

    def place_of(slot, at_half):
        return attended.at[
            pl.ds(pl.multiple_of(at_half * half, half), half),
            pl.ds(pl.multiple_of(slot * 128, 128), 128),
        ]

    def out_copy(s, piece):
        to_z, to_half = chunk_of(s, piece % 2)
        plane = y_low if piece < 2 else 1 - y_low
        return remote(
            out_stage.at[s, piece], place_of(slot_of_mine, to_half), out_send.at[s, piece],
            out_recv.at[s, piece], to_z * 2 + plane, grp,
        )

    def finish(s):
        one, other = (mix[m, s] / pltpu.roll(mix[m, s], 64, 1) for m in range(2))
        packed = jnp.where(lane < 64, pltpu.roll(one, 64, 1), other).astype(jnp.bfloat16)

        @pl.when(s > 0)
        def _():
            for piece in range(2):
                out_stage[s, piece] = packed[piece * half : (piece + 1) * half]
                out_copy(s, piece).start()

        @pl.when(s == 0)
        def _():
            mine = pl.ds(pl.multiple_of(slot_of_mine * 128, 128), 128)
            attended[:rows, mine] = packed[:rows]

        for piece in range(2, 4):
            out_stage[s, piece] = packed[piece * half : (piece + 1) * half]
            out_copy(s, piece).start()

    last = SETS - 1
    arrange(last)
    buf_a[...] = score(0, *pair(last, 0))

    def release(p, carry):
        both_heads(last, p)
        finish(pair(last, p)[0])
        return carry

    lax.fori_loop(0, NEAR - 1, release, 0)
    last_heads(last, NEAR - 1)
    finish(0)
    for item in loads[5:]:
        item.wait()

    def collect(s, carry):
        for piece in range(4):
            plane = y_low if piece < 2 else 1 - y_low
            from_z, _ = chunk_of(s, 1 - piece % 2)
            _, at_half = chunk_of(s, piece % 2)
            got = remote(
                out_stage.at[s, piece], place_of(from_z % 4 * 2 + plane, at_half),
                out_send.at[s, piece], out_recv.at[s, piece], from_z * 2 + plane, grp,
            )

            def settle(got=got):
                got.wait_recv()
                got.wait_send()

            if piece < 2:
                pl.when(s > 0)(settle)
            else:
                settle()
        return carry

    lax.fori_loop(0, NEAR, collect, 0)

    frames = jnp.concatenate([from_low[7], from_high[7]], axis=0).astype(jnp.float32)
    added = (
        frames + jnp.dot(attended[...], w_out[...], preferred_element_type=jnp.float32)
    ).astype(jnp.bfloat16)
    residual[...] = added
    conv_in = normalize(added.astype(jnp.float32), conv_gain[...]).astype(jnp.bfloat16)
    width = added.shape[1]
    columns = width // 128
    for column in range(0, width, 256):
        values = jnp.dot(
            conv_in, w_glu[:, column : column + 256], preferred_element_type=jnp.float32
        )
        gates = jnp.dot(
            conv_in, w_glu[:, width + column : width + column + 256],
            preferred_element_type=jnp.float32,
        )
        gated = (values * jax.nn.sigmoid(gates)).astype(jnp.bfloat16)
        edge_out[0, :, column : column + 256] = gated[:HALO]
        edge_out[1, :, column : column + 256] = gated[rows - HALO :]
        wide = gated.astype(jnp.float32)
        for c in range(2):
            tall[column // 128 + c, HALO : HALO + rows] = wide[:, c * 128 : (c + 1) * 128]

    to_left = remote(edge_out.at[0], edge_in.at[1], halo_send.at[0], halo_recv.at[0], *left)
    to_right = remote(edge_out.at[1], edge_in.at[0], halo_send.at[1], halo_recv.at[1], *right)
    to_left.start()
    to_right.start()

    taps = w_depth.shape[0]
    reach = taps // 2
    block = 64
    first_frame = (grp * 16 + blk) * rows

    def convolve(base):
        at = lax.broadcasted_iota(jnp.int32, (block, 128), 0) + (first_frame + base)
        first = jnp.zeros((block, 128), jnp.int32)
        final = jnp.zeros((block, 128), jnp.int32)
        begun = jnp.int32(0)
        for c in range(8):
            over = begun + utt[c]
            first = jnp.where(at >= begun, begun, first)
            final = jnp.where(at >= begun, over, final)
            begun = over
        first_tap = first - at + reach
        last_tap = final - at + reach
        for t in range(taps):
            valid[t] = jnp.where((first_tap <= t) & (last_tap > t), 1.0, 0.0)

        def column_of(c, carry):
            total = jnp.zeros((block, 128), jnp.float32)
            for t in range(taps):
                total = total + (
                    tall[c, pl.ds(base + (HALO - reach + t), block)] * valid[t]
                    * w_depth[t : t + 1, pl.ds(pl.multiple_of(c * 128, 128), 128)]
                )
            mixed[c] = total
            return carry

        lax.fori_loop(0, columns, column_of, 0)
        pieces = [mixed[c] for c in range(columns)]
        mean = jnp.sum(functools.reduce(jnp.add, pieces), axis=1, keepdims=True) / width
        pieces = [piece - mean for piece in pieces]
        spread = (
            jnp.sum(functools.reduce(jnp.add, [p * p for p in pieces]), axis=1, keepdims=True)
            / width
        )
        factor = lax.rsqrt(spread + epsilon)
        for c in range(columns):
            span = slice(c * 128, (c + 1) * 128)
            value = pieces[c] * factor * depth_gain[:, span]
            activated[pl.ds(base, block), span] = (value * jax.nn.sigmoid(value)).astype(
                jnp.bfloat16
            )

    def conv_step(index, carry):
        @pl.when(index == rows // block - 2)
        def _():
            to_left.wait_recv()
            to_right.wait_recv()
            for c in range(columns):
                span = slice(c * 128, (c + 1) * 128)
                tall[c, :HALO] = edge_in[0, :, span].astype(jnp.float32)
                tall[c, HALO + rows :] = edge_in[1, :, span].astype(jnp.float32)

        convolve(pl.multiple_of((index + 1) % (rows // block) * block, block))
        return carry

    lax.fori_loop(0, rows // block, conv_step, 0)
    for column in range(0, width, 256):
        span = slice(column, column + 256)
        out_ref[:, span] = (
            residual[:, span].astype(jnp.float32)
            + jnp.dot(activated[...], w_proj[:, span], preferred_element_type=jnp.float32)
        ).astype(jnp.bfloat16)

    for event in range(7):
        low_copy(event, from_low.at[event]).wait_send()
        high_copy(event, from_high.at[event]).wait_send()
    for s in range(SETS):
        kv_copy(s).wait_send()
    for s in range(NEAR):
        q_copy(s).wait_send()
    for item in core_copies(core):
        item.wait_send()

    def sent_w(m):
        for item in w_copies(m):
            item.wait_send()

    for m in range(2):
        unless_own(m, functools.partial(sent_w, m))
    to_left.wait_send()
    to_right.wait_send()


def block_of(
    frames, utt_lengths, attn_gain, w_qkv, w_out, conv_gain, w_glu, w_depth, depth_gain, w_proj
):
    rows, width = frames.shape
    half = rows // 2
    columns = width // 128
    taps = w_depth.shape[0]
    hbm = pl.BlockSpec(memory_space=pltpu.HBM)
    dma = pltpu.SemaphoreType.DMA
    bf16, f32 = jnp.bfloat16, jnp.float32
    return pl.pallas_call(
        mixing_kernel,
        out_shape=jax.ShapeDtypeStruct((rows, width), bf16),
        in_specs=[hbm] * 10,
        out_specs=pl.BlockSpec(memory_space=pltpu.VMEM),
        scratch_shapes=[
            pltpu.SMEM((8,), jnp.int32),
            pltpu.VMEM((1, width), f32),
            pltpu.VMEM((1, width), f32),
            pltpu.VMEM((1, width), f32),
            pltpu.VMEM((192, width), bf16),
            pltpu.VMEM((width, width), bf16),
            pltpu.VMEM((width, 2 * width), bf16),
            pltpu.VMEM((taps, width), f32),
            pltpu.VMEM((width, width), bf16),
            pltpu.VMEM((8, half, width), bf16),
            pltpu.VMEM((8, half, width), bf16),
            pltpu.VMEM((2, 256, width), bf16),
            pltpu.VMEM((2, 128, width), bf16),
            pltpu.VMEM((SETS, rows, 256), bf16),
            pltpu.VMEM((NEAR, rows, 128), bf16),
            pltpu.VMEM((SETS, 2 * rows, 256), bf16),
            pltpu.VMEM((NEAR, 2 * rows, 128), bf16),
            pltpu.VMEM((2, NEAR, 2 * rows, 128), bf16),
            pltpu.VMEM((2, SETS, 2 * rows, 128), bf16),
            pltpu.VMEM((2, SETS, 2 * rows, 128), bf16),
            pltpu.VMEM((2, NEAR, 2 * rows, 128), f32),
            pltpu.VMEM((2, NEAR, 2 * rows, 128), f32),
            pltpu.VMEM((2 * rows, 2 * rows), f32),
            pltpu.VMEM((2 * rows, 2 * rows), f32),
            pltpu.VMEM((NEAR, 4, half, 128), bf16),
            pltpu.VMEM((rows, width), bf16),
            pltpu.VMEM((rows, width), bf16),
            pltpu.VMEM((rows, width), bf16),
            pltpu.VMEM((2, HALO, width), bf16),
            pltpu.VMEM((2, HALO, width), bf16),
            pltpu.VMEM((columns, rows + 2 * HALO, 128), f32),
            pltpu.VMEM((taps, 64, 128), f32),
            pltpu.VMEM((columns, 64, 128), f32),
            dma((26,)),
            dma((7,)), dma((7,)), dma((7,)), dma((7,)),
            dma((2, 2)), dma((2, 2)), dma((2,)), dma((2,)),
            dma((SETS,)), dma((SETS,)), dma((NEAR,)), dma((NEAR,)),
            dma((NEAR, 4)), dma((NEAR, 4)),
            dma((2,)), dma((2,)),
        ],
        compiler_params=pltpu.CompilerParams(
            collective_id=0, has_side_effects=True, vmem_limit_bytes=67043328
        ),
    )(
        utt_lengths, frames, attn_gain.reshape(1, width), w_qkv.T, w_out,
        conv_gain.reshape(1, width), w_glu, w_depth, depth_gain.reshape(1, width), w_proj,
    )


def body(frames, *others):
    return block_of(frames[0], *others)[None]


def solution(mesh):
    in_specs = (P("grp", "blk", None), P(), P(), P(None, "grp"), P(), P(), P(), P(), P(), P())
    out_specs = P("grp", "blk", None)
    return jax.shard_map(body, mesh=mesh, in_specs=in_specs, out_specs=out_specs, check_vma=False)
```

time: 92.3 us -> 96.9 us (1.050)
  Pallas kernels: 90.3 us -> 94.9 us
    pallas_call x1, Pallas kernels: 90.3 us -> 94.9 us  [block_of(): pl.pallas_call(mixing_kernel, out_shape=jax.ShapeDtypeStruct((rows, width...]
where the time goes in v4:
time: 96.9 us; the launch traced here: 96.7 us
  Pallas kernels  94.9 us (98%)
  local copies, waits for them, and re-layouts  1.87 us (2%)
    pallas_call x1, Pallas kernels, block_of(): pl.pallas_call(mixing_kernel, out_shape=jax.ShapeDtypeStruct((rows, width...  94.9 us

profile of v4, /device:TPU:1, one launch (start us, length us, event | category | flops | bytes accessed | tf_op | source)
XLA Modules:
  0.0 96.7 jit_solution(8407309884475542662)
XLA Ops:
  0.0 94.9 %shard_map.100 = bf16[256,1024]{1,0:T(8,128)(2,1)} custom-call(s32[8]{0:T(128)} %utt_hbm.1, bf16[256,1024]{1,0:T(8,128)(2,1)} %bitcast.7, f32[1,1024]{1,0:T(1,128)} %bitcast.9, bf16[192,1024]{1,0:T(8,128)(2,1)} %bitcast.8, bf16[1024,1024]{1,0:T(8,128)(2,1)} %w_out_hbm.1, f32[1,1024]{1,0:T(1,128)} %bitcast.10, bf16[1024,2048]{1,0:T(8,128)(2,1)} %w_glu_hbm.1, ...), custom_call_target="tpu_custom_call" | custom-call | tf_op jit(solution)/shard_map/pallas_call | solution.py:556
  94.9 1.9 %copy.12 = bf16[1,256,1024]{2,1,0:T(8,128)(2,1)} copy(bf16[1,256,1024]{2,1,0:T(8,128)(2,1)} %bitcast.6) | data formatting | bytes 1048576

commit v5 on v4

--- a/solution.py
+++ b/solution.py
@@ -29,9 +29,10 @@
     depth_gain_hbm, w_proj_hbm,
     out_ref,
     utt, gain, conv_gain, depth_gain, w_mine, w_out, w_glu, w_depth, w_proj,
-    from_low, from_high, w_kv, w_q, kv_stage, q_stage, kv_land, q_land, query, keys, vals,
+    own, from_low, from_high, w_relay, w_kv, w_q, kv_stage, q_stage, kv_land, q_land, query, keys, vals,
     peak, mix, buf_a, buf_b, out_stage, attended, activated, residual, edge_out, edge_in, tall, valid, mixed,
-    load_sem, low_send, low_recv, high_send, high_recv, w_send, w_recv, core_send, core_recv,
+    load_sem, low_send, low_recv, high_send, high_recv, w_send, w_recv, relay_send, relay_recv,
+    far_send, core_send, core_recv,
     kv_send, kv_recv, q_send, q_recv, out_send, out_recv, halo_send, halo_recv,
 ):
     half = from_low.shape[1]
@@ -43,8 +44,7 @@
     quad = z % 4
 
     def member(of_quad, m):
-        odd = of_quad % 2
-        return jnp.where(odd == 1, of_quad, 2 * m), jnp.where(odd == 1, m, of_quad // 2)
+        return (of_quad + 2 * m) % 4, m
 
     def head_of(of_quad, m, of_core):
         right_by, across = member(of_quad, m)
@@ -63,11 +63,28 @@
             ((x + 4 - right_by) % 4) * 4 + ((y_high + across) % 2) * 2 + core,
         )
 
-    def unless_own(m, act):
+    even = quad % 2 == 0
+    far = jnp.where(quad == 0, 1, 0)
+    stride = jnp.where(core == 0, 3, 1)
+
+    def along(count, across):
+        return (
+            jnp.where(across == 1, partner, blk),
+            ((x + count) % 4) * 4 + ((y_high + across) % 2) * 2 + core,
+        )
+
+    relay_to, relay_from = along(stride, 0), along(4 - stride, 0)
+    far_to, far_from = along(stride, far), along(4 - stride, far)
+
+    def if_direct(m, act):
+        pl.when(quad > 0 if m == 1 else quad % 2 == 1)(act)
+
+    def if_sent(m, act):
         if m == 1:
             act()
         else:
             pl.when(quad > 0)(act)
+
     z_up = (blk + 2) % 16
     z_down = (blk + 14) % 16
     left = ((blk + 15) % 16, (grp + jnp.where(blk == 0, 15, 0)) % 16)
@@ -80,12 +97,11 @@
         return pltpu.make_async_copy(src, dst, load_sem.at[index])
 
     loads = [
-        load(0, frames_hbm.at[pl.ds(0, half)], from_low.at[7]),
-        load(1, frames_hbm.at[pl.ds(half, half)], from_high.at[7]),
+        load(0, frames_hbm, own),
+        load(1, conv_gain_hbm, conv_gain),
         load(2, w_hbm, w_mine),
         load(3, gain_hbm, gain),
         load(4, utt_hbm, utt),
-        load(5, conv_gain_hbm, conv_gain),
         load(7, w_glu_hbm, w_glu),
         load(8, w_depth_hbm, w_depth),
         load(9, depth_gain_hbm, depth_gain),
@@ -120,9 +136,21 @@
             greet(*w_to(m))
             greet(*w_from(m))
 
-        unless_own(m, greet_both)
-
-    pl.semaphore_wait(barrier, jnp.where(quad > 0, 22, 20))
+        if_direct(m, greet_both)
+
+    @pl.when(even)
+    def _():
+        for each in (relay_to, relay_from, far_to, far_from):
+            greet(*each)
+
+    loads[0].wait()
+    loads[3].wait()
+    for side, kept in ((0, from_low), (1, from_high)):
+        kept[7] = normalize(
+            own[side * half : (side + 1) * half].astype(jnp.float32), gain[...]
+        ).astype(jnp.bfloat16)
+    loads[2].wait()
+    pl.semaphore_wait(barrier, jnp.where(quad == 2, 24, 22))
 
     def remote(src, dst, send, recv, b, g):
         return pltpu.make_async_remote_copy(
@@ -138,13 +166,10 @@
             src, from_high.at[event], high_send.at[event], high_recv.at[event], z_down, grp
         )
 
-    loads[0].wait()
-    loads[1].wait()
     low_copy(0, from_low.at[7]).start()
     high_copy(0, from_high.at[7]).start()
     low_copy(1, from_high.at[7]).start()
     high_copy(1, from_low.at[7]).start()
-    loads[2].wait()
 
     def w_copies(m):
         return (
@@ -162,15 +187,47 @@
         for item in w_copies(m):
             item.start()
 
+    def relay_copies():
+        return [
+            remote(
+                w_mine.at[at], w_relay.at[at], relay_send.at[part], relay_recv.at[part], *relay_to
+            )
+            for part, at in enumerate((pl.ds(64, 128), pl.ds(0, 64)))
+        ]
+
+    def far_copies():
+        return (
+            remote(
+                w_relay.at[pl.ds(64, 128)],
+                w_kv.at[core, pl.ds(pl.multiple_of(far * 128, 128), 128)],
+                far_send.at[0], w_recv.at[far, 0], *far_to,
+            ),
+            remote(
+                w_relay.at[pl.ds(0, 64)],
+                w_q.at[core, pl.ds(pl.multiple_of(far * 64, 64), 64)],
+                far_send.at[1], w_recv.at[far, 1], *far_to,
+            ),
+        )
+
+    @pl.when(even)
+    def _():
+        for item in relay_copies():
+            item.start()
+
     for m in range(2):
-        unless_own(m, functools.partial(start_w, m))
+        if_direct(m, functools.partial(start_w, m))
 
     @pl.when(quad == 0)
     def _():
         w_kv[core, :128] = w_mine[64:]
         w_q[core, :64] = w_mine[:64]
 
-    loads[3].wait()
+    @pl.when(even)
+    def _():
+        for came, item in zip(relay_copies(), far_copies()):
+            came.wait_recv()
+            item.start()
+
     loads[4].wait()
 
     def arrive(event):
@@ -187,14 +244,13 @@
             high_copy(event + 2, from_high.at[event]).start()
 
     arrive(0)
-    arrive(1)
 
     def await_w(m):
         for item in w_copies(m):
             item.wait_recv()
 
     for m in range(2):
-        unless_own(m, functools.partial(await_w, m))
+        if_sent(m, functools.partial(await_w, m))
 
     def core_copies(which):
         return (
@@ -247,8 +303,7 @@
 
     def project(s):
         slot = (s + 7) % 8
-        frames = jnp.concatenate([from_low[slot], from_high[slot]], axis=0).astype(jnp.float32)
-        normed = normalize(frames, gain[...]).astype(jnp.bfloat16)
+        normed = jnp.concatenate([from_low[slot], from_high[slot]], axis=0)
         kv_stage[s] = times(normed, w_kv[1 - y_low]).astype(jnp.bfloat16)
         kv_copy(s).start()
 
@@ -341,20 +396,22 @@
         last_heads(s, count - 1)
 
     def step(s, carry):
-        @pl.when(s >= 3)
+        @pl.when((s >= 2) & (s < SETS))
         def _():
             arrive(s - 1)
 
-        project(s)
-
-        @pl.when(s >= 1)
-        def _():
-            arrange(s - 1)
-            attend(s - 1)
+        @pl.when(s < SETS)
+        def _():
+            project(s)
+
+        @pl.when(s >= 2)
+        def _():
+            arrange(s - 2)
+            attend(s - 2)
 
         return carry
 
-    lax.fori_loop(0, SETS, step, 0)
+    lax.fori_loop(0, SETS + 1, step, 0)
 
     slot_of_mine = quad * 2 + y_low
 
@@ -403,7 +460,7 @@
     lax.fori_loop(0, NEAR - 1, release, 0)
     last_heads(last, NEAR - 1)
     finish(0)
-    for item in loads[5:]:
+    for item in loads[1:2] + loads[5:]:
         item.wait()
 
     def collect(s, carry):
@@ -428,9 +485,8 @@
 
     lax.fori_loop(0, NEAR, collect, 0)
 
-    frames = jnp.concatenate([from_low[7], from_high[7]], axis=0).astype(jnp.float32)
     added = (
-        frames + jnp.dot(attended[...], w_out[...], preferred_element_type=jnp.float32)
+        own[...].astype(jnp.float32) + jnp.dot(attended[...], w_out[...], preferred_element_type=jnp.float32)
     ).astype(jnp.bfloat16)
     residual[...] = added
     conv_in = normalize(added.astype(jnp.float32), conv_gain[...]).astype(jnp.bfloat16)
@@ -538,7 +594,13 @@
             item.wait_send()
 
     for m in range(2):
-        unless_own(m, functools.partial(sent_w, m))
+        if_direct(m, functools.partial(sent_w, m))
+
+    @pl.when(even)
+    def _():
+        for item in (*relay_copies(), *far_copies()):
+            item.wait_send()
+
     to_left.wait_send()
     to_right.wait_send()
 
@@ -568,8 +630,10 @@
             pltpu.VMEM((width, 2 * width), bf16),
             pltpu.VMEM((taps, width), f32),
             pltpu.VMEM((width, width), bf16),
+            pltpu.VMEM((rows, width), bf16),
             pltpu.VMEM((8, half, width), bf16),
             pltpu.VMEM((8, half, width), bf16),
+            pltpu.VMEM((192, width), bf16),
             pltpu.VMEM((2, 256, width), bf16),
             pltpu.VMEM((2, 128, width), bf16),
             pltpu.VMEM((SETS, rows, 256), bf16),
@@ -594,7 +658,7 @@
             pltpu.VMEM((columns, 64, 128), f32),
             dma((26,)),
             dma((7,)), dma((7,)), dma((7,)), dma((7,)),
-            dma((2, 2)), dma((2, 2)), dma((2,)), dma((2,)),
+            dma((2, 2)), dma((2, 2)), dma((2,)), dma((2,)), dma((2,)), dma((2,)), dma((2,)),
             dma((SETS,)), dma((SETS,)), dma((NEAR,)), dma((NEAR,)),
             dma((NEAR, 4)), dma((NEAR, 4)),
             dma((2,)), dma((2,)),

time: 96.9 us -> 88.1 us (0.909)
  Pallas kernels: 94.9 us -> 86.1 us
    pallas_call x1, Pallas kernels: 94.9 us -> 86.1 us  [block_of(): pl.pallas_call(mixing_kernel, out_shape=jax.ShapeDtypeStruct((rows, width...]
where the time goes in v5:
time: 88.1 us; the launch traced here: 87.9 us
  Pallas kernels  86.1 us (98%)
  local copies, waits for them, and re-layouts  1.87 us (2%)
    pallas_call x1, Pallas kernels, block_of(): pl.pallas_call(mixing_kernel, out_shape=jax.ShapeDtypeStruct((rows, width...  86.1 us
    unnamed x1, local copies, waits for them, and re-layouts  1.87 us

profile of v5, /device:TPU:1, one launch (start us, length us, event | category | flops | bytes accessed | tf_op | source)
XLA Modules:
  0.0 87.9 jit_solution(236694963504956311)
XLA Ops:
  0.0 86.1 %shard_map.100 = bf16[256,1024]{1,0:T(8,128)(2,1)} custom-call(s32[8]{0:T(128)} %utt_hbm.1, bf16[256,1024]{1,0:T(8,128)(2,1)} %bitcast.7, f32[1,1024]{1,0:T(1,128)} %bitcast.9, bf16[192,1024]{1,0:T(8,128)(2,1)} %bitcast.8, bf16[1024,1024]{1,0:T(8,128)(2,1)} %w_out_hbm.1, f32[1,1024]{1,0:T(1,128)} %bitcast.10, bf16[1024,2048]{1,0:T(8,128)(2,1)} %w_glu_hbm.1, ...), custom_call_target="tpu_custom_call" | custom-call | tf_op jit(solution)/shard_map/pallas_call | solution.py:618
  86.1 1.9 %copy.12 = bf16[1,256,1024]{2,1,0:T(8,128)(2,1)} copy(bf16[1,256,1024]{2,1,0:T(8,128)(2,1)} %bitcast.6) | data formatting | bytes 1048576

commit v6 on v5

--- a/solution.py
+++ b/solution.py
@@ -330,7 +330,7 @@
             for m in range(2):
                 both = kv_land[s, span, m * 128 : (m + 1) * 128].astype(jnp.float32)
                 keys[m, s, span] = jnp.where(lane < 64, both, inside).astype(jnp.bfloat16)
-                vals[m, s, span] = jnp.where(lane < 64, 1.0, both).astype(jnp.bfloat16)
+                vals[m, s, :, span] = jnp.where(lane < 64, 1.0, both).T.astype(jnp.bfloat16)
 
         @pl.when(s < NEAR)
         def _():
@@ -344,23 +344,18 @@
                     jnp.bfloat16
                 )
             for m in range(2):
-                peak[m, s] = jnp.full((2 * rows, 128), lowest, jnp.float32)
-                mix[m, s] = jnp.zeros((2 * rows, 128), jnp.float32)
+                peak[m, s] = jnp.full((1, 2 * rows), lowest, jnp.float32)
+                mix[m, s] = jnp.zeros((128, 2 * rows), jnp.float32)
 
     def score(m, q, k):
-        return times(query[m, q], keys[m, k])
+        return times(keys[m, k], query[m, q])
 
     def absorb(m, q, k, buf):
-        tiles = [buf[:, t * 128 : (t + 1) * 128] for t in range(2 * rows // 128)]
         old = peak[m, q]
-        new = jnp.maximum(
-            old, jnp.max(functools.reduce(jnp.maximum, tiles), axis=1, keepdims=True)
-        )
-        weights = jnp.concatenate(
-            [jnp.exp2(tile - new).astype(jnp.bfloat16) for tile in tiles], axis=1
-        )
+        new = jnp.maximum(old, jnp.max(buf[...], axis=0, keepdims=True))
+        weights = jnp.exp2(buf[...] - new).astype(jnp.bfloat16)
         mix[m, q] = mix[m, q] * jnp.exp2(old - new) + jnp.dot(
-            weights, vals[m, k], preferred_element_type=jnp.float32
+            vals[m, k], weights, preferred_element_type=jnp.float32
         )
         peak[m, q] = new
 
@@ -430,8 +425,9 @@
         )
 
     def finish(s):
-        one, other = (mix[m, s] / pltpu.roll(mix[m, s], 64, 1) for m in range(2))
-        packed = jnp.where(lane < 64, pltpu.roll(one, 64, 1), other).astype(jnp.bfloat16)
+        packed = jnp.concatenate(
+            [mix[m, s, 64:] / mix[m, s, :1] for m in range(2)], axis=0
+        ).T.astype(jnp.bfloat16)
 
         @pl.when(s > 0)
         def _():
@@ -642,9 +638,9 @@
             pltpu.VMEM((NEAR, 2 * rows, 128), bf16),
             pltpu.VMEM((2, NEAR, 2 * rows, 128), bf16),
             pltpu.VMEM((2, SETS, 2 * rows, 128), bf16),
-            pltpu.VMEM((2, SETS, 2 * rows, 128), bf16),
-            pltpu.VMEM((2, NEAR, 2 * rows, 128), f32),
-            pltpu.VMEM((2, NEAR, 2 * rows, 128), f32),
+            pltpu.VMEM((2, SETS, 128, 2 * rows), bf16),
+            pltpu.VMEM((2, NEAR, 1, 2 * rows), f32),
+            pltpu.VMEM((2, NEAR, 128, 2 * rows), f32),
             pltpu.VMEM((2 * rows, 2 * rows), f32),
             pltpu.VMEM((2 * rows, 2 * rows), f32),
             pltpu.VMEM((NEAR, 4, half, 128), bf16),

time: 88.1 us -> 84.9 us (0.964)
  Pallas kernels: 86.1 us -> 82.7 us
    pallas_call x1, Pallas kernels: 86.1 us -> 82.7 us  [block_of(): pl.pallas_call(mixing_kernel, out_shape=jax.ShapeDtypeStruct((rows, width...]
where the time goes in v6:
time: 84.9 us; the launch traced here: 84.6 us
  Pallas kernels  82.7 us (97%)
  local copies, waits for them, and re-layouts  1.87 us (2%)
    pallas_call x1, Pallas kernels, block_of(): pl.pallas_call(mixing_kernel, out_shape=jax.ShapeDtypeStruct((rows, width...  82.7 us
    unnamed x1, local copies, waits for them, and re-layouts  1.87 us

profile of v6, /device:TPU:1, one launch (start us, length us, event | category | flops | bytes accessed | tf_op | source)
XLA Modules:
  0.0 84.6 jit_solution(3237057111132000357)
XLA Ops:
  0.0 82.7 %shard_map.100 = bf16[256,1024]{1,0:T(8,128)(2,1)} custom-call(s32[8]{0:T(128)} %utt_hbm.1, bf16[256,1024]{1,0:T(8,128)(2,1)} %bitcast.7, f32[1,1024]{1,0:T(1,128)} %bitcast.9, bf16[192,1024]{1,0:T(8,128)(2,1)} %bitcast.8, bf16[1024,1024]{1,0:T(8,128)(2,1)} %w_out_hbm.1, f32[1,1024]{1,0:T(1,128)} %bitcast.10, bf16[1024,2048]{1,0:T(8,128)(2,1)} %w_glu_hbm.1, ...), custom_call_target="tpu_custom_call" | custom-call | tf_op jit(solution)/shard_map/pallas_call | solution.py:614
  82.7 1.9 %copy.12 = bf16[1,256,1024]{2,1,0:T(8,128)(2,1)} copy(bf16[1,256,1024]{2,1,0:T(8,128)(2,1)} %bitcast.6) | data formatting | bytes 1048576

commit v7 on v6

--- a/solution.py
+++ b/solution.py
@@ -459,62 +459,13 @@
     for item in loads[1:2] + loads[5:]:
         item.wait()
 
-    def collect(s, carry):
-        for piece in range(4):
-            plane = y_low if piece < 2 else 1 - y_low
-            from_z, _ = chunk_of(s, 1 - piece % 2)
-            _, at_half = chunk_of(s, piece % 2)
-            got = remote(
-                out_stage.at[s, piece], place_of(from_z % 4 * 2 + plane, at_half),
-                out_send.at[s, piece], out_recv.at[s, piece], from_z * 2 + plane, grp,
-            )
-
-            def settle(got=got):
-                got.wait_recv()
-                got.wait_send()
-
-            if piece < 2:
-                pl.when(s > 0)(settle)
-            else:
-                settle()
-        return carry
-
-    lax.fori_loop(0, NEAR, collect, 0)
-
-    added = (
-        own[...].astype(jnp.float32) + jnp.dot(attended[...], w_out[...], preferred_element_type=jnp.float32)
-    ).astype(jnp.bfloat16)
-    residual[...] = added
-    conv_in = normalize(added.astype(jnp.float32), conv_gain[...]).astype(jnp.bfloat16)
-    width = added.shape[1]
-    columns = width // 128
-    for column in range(0, width, 256):
-        values = jnp.dot(
-            conv_in, w_glu[:, column : column + 256], preferred_element_type=jnp.float32
-        )
-        gates = jnp.dot(
-            conv_in, w_glu[:, width + column : width + column + 256],
-            preferred_element_type=jnp.float32,
-        )
-        gated = (values * jax.nn.sigmoid(gates)).astype(jnp.bfloat16)
-        edge_out[0, :, column : column + 256] = gated[:HALO]
-        edge_out[1, :, column : column + 256] = gated[rows - HALO :]
-        wide = gated.astype(jnp.float32)
-        for c in range(2):
-            tall[column // 128 + c, HALO : HALO + rows] = wide[:, c * 128 : (c + 1) * 128]
-
-    to_left = remote(edge_out.at[0], edge_in.at[1], halo_send.at[0], halo_recv.at[0], *left)
-    to_right = remote(edge_out.at[1], edge_in.at[0], halo_send.at[1], halo_recv.at[1], *right)
-    to_left.start()
-    to_right.start()
-
     taps = w_depth.shape[0]
     reach = taps // 2
     block = 64
     first_frame = (grp * 16 + blk) * rows
 
-    def convolve(base):
-        at = lax.broadcasted_iota(jnp.int32, (block, 128), 0) + (first_frame + base)
+    def mark_taps(part, carry):
+        at = lax.broadcasted_iota(jnp.int32, (block, 128), 0) + (first_frame + part * block)
         first = jnp.zeros((block, 128), jnp.int32)
         final = jnp.zeros((block, 128), jnp.int32)
         begun = jnp.int32(0)
@@ -526,13 +477,66 @@
         first_tap = first - at + reach
         last_tap = final - at + reach
         for t in range(taps):
-            valid[t] = jnp.where((first_tap <= t) & (last_tap > t), 1.0, 0.0)
-
+            valid[part, t] = jnp.where((first_tap <= t) & (last_tap > t), 1.0, 0.0)
+        return carry
+
+    lax.fori_loop(0, rows // block, mark_taps, 0)
+
+    def collect(s, carry):
+        for piece in range(4):
+            plane = y_low if piece < 2 else 1 - y_low
+            from_z, _ = chunk_of(s, 1 - piece % 2)
+            _, at_half = chunk_of(s, piece % 2)
+            got = remote(
+                out_stage.at[s, piece], place_of(from_z % 4 * 2 + plane, at_half),
+                out_send.at[s, piece], out_recv.at[s, piece], from_z * 2 + plane, grp,
+            )
+
+            def settle(got=got):
+                got.wait_recv()
+                got.wait_send()
+
+            if piece < 2:
+                pl.when(s > 0)(settle)
+            else:
+                settle()
+        return carry
+
+    lax.fori_loop(0, NEAR, collect, 0)
+
+    added = (
+        own[...].astype(jnp.float32) + jnp.dot(attended[...], w_out[...], preferred_element_type=jnp.float32)
+    ).astype(jnp.bfloat16)
+    residual[...] = added
+    conv_in = normalize(added.astype(jnp.float32), conv_gain[...]).astype(jnp.bfloat16)
+    width = added.shape[1]
+    columns = width // 128
+    for column in range(0, width, 256):
+        values = jnp.dot(
+            conv_in, w_glu[:, column : column + 256], preferred_element_type=jnp.float32
+        )
+        gates = jnp.dot(
+            conv_in, w_glu[:, width + column : width + column + 256],
+            preferred_element_type=jnp.float32,
+        )
+        gated = (values * jax.nn.sigmoid(gates)).astype(jnp.bfloat16)
+        edge_out[0, :, column : column + 256] = gated[:HALO]
+        edge_out[1, :, column : column + 256] = gated[rows - HALO :]
+        wide = gated.astype(jnp.float32)
+        for c in range(2):
+            tall[column // 128 + c, HALO : HALO + rows] = wide[:, c * 128 : (c + 1) * 128]
+
+    to_left = remote(edge_out.at[0], edge_in.at[1], halo_send.at[0], halo_recv.at[0], *left)
+    to_right = remote(edge_out.at[1], edge_in.at[0], halo_send.at[1], halo_recv.at[1], *right)
+    to_left.start()
+    to_right.start()
+
+    def convolve(base):
         def column_of(c, carry):
             total = jnp.zeros((block, 128), jnp.float32)
             for t in range(taps):
                 total = total + (
-                    tall[c, pl.ds(base + (HALO - reach + t), block)] * valid[t]
+                    tall[c, pl.ds(base + (HALO - reach + t), block)] * valid[base // block, t]
                     * w_depth[t : t + 1, pl.ds(pl.multiple_of(c * 128, 128), 128)]
                 )
             mixed[c] = total
@@ -650,7 +654,7 @@
             pltpu.VMEM((2, HALO, width), bf16),
             pltpu.VMEM((2, HALO, width), bf16),
             pltpu.VMEM((columns, rows + 2 * HALO, 128), f32),
-            pltpu.VMEM((taps, 64, 128), f32),
+            pltpu.VMEM((rows // 64, taps, 64, 128), f32),
             pltpu.VMEM((columns, 64, 128), f32),
             dma((26,)),
             dma((7,)), dma((7,)), dma((7,)), dma((7,)),

time: 84.9 us -> 84.6 us (level)
  no operation moved by 1% of the time
where the time goes in v7:
time: 84.6 us; the launch traced here: 84.3 us
  Pallas kernels  82.4 us (97%)
  local copies, waits for them, and re-layouts  1.87 us (2%)
    pallas_call x1, Pallas kernels, block_of(): pl.pallas_call(mixing_kernel, out_shape=jax.ShapeDtypeStruct((rows, width...  82.4 us
    unnamed x1, local copies, waits for them, and re-layouts  1.87 us

profile of v7, /device:TPU:1, one launch (start us, length us, event | category | flops | bytes accessed | tf_op | source)
XLA Modules:
  0.0 84.3 jit_solution(9730859833738547311)
XLA Ops:
  0.0 82.4 %shard_map.100 = bf16[256,1024]{1,0:T(8,128)(2,1)} custom-call(s32[8]{0:T(128)} %utt_hbm.1, bf16[256,1024]{1,0:T(8,128)(2,1)} %bitcast.7, f32[1,1024]{1,0:T(1,128)} %bitcast.9, bf16[192,1024]{1,0:T(8,128)(2,1)} %bitcast.8, bf16[1024,1024]{1,0:T(8,128)(2,1)} %w_out_hbm.1, f32[1,1024]{1,0:T(1,128)} %bitcast.10, bf16[1024,2048]{1,0:T(8,128)(2,1)} %w_glu_hbm.1, ...), custom_call_target="tpu_custom_call" | custom-call | tf_op jit(solution)/shard_map/pallas_call | solution.py:618
  82.5 1.9 %copy.12 = bf16[1,256,1024]{2,1,0:T(8,128)(2,1)} copy(bf16[1,256,1024]{2,1,0:T(8,128)(2,1)} %bitcast.6) | data formatting | bytes 1048576
